TPU v7x, 32 devices: a whole 2x2x4 slice. The times are simulated.
32 devices in a mesh: freq: 2 (over x), param: 4 (over y, core), sens: 4 (over z).
Axes of the slice: x: 2, y: 2, z: 4, core: 2. Of those that a mesh axis runs over, the one named last changes fastest.
Arguments:
- series: bfloat16 [8, 600, 52], P(None, 'sens', 'freq'), may hold values from -6 to 6
- kernel: bfloat16 [2, 32, 600, 4096], P(None, 'freq', 'sens', 'param'), may hold values from -0.1875 to 0.1875
- prior_spectrum: float32 [32], P('freq'), may hold values from 0.3 to 1.5
- prior_scale: float32 [4096], P('param'), may hold values from 0.5 to 2
Outputs:
- adjoint_map: float32 [52, 8, 4096], P('freq', 'sens', 'param')
All inputs are finite; a program needn't handle non-finite values.
Results may differ from a plain program's by a relative error of at most 0.0047.
Values may be sent and summed in bfloat16 or wider, within the bound.
A program may use at most 64 MiB of HBM per device.

v0:
```python
import functools
import math

import jax
import jax.numpy as jnp
import numpy as np
from jax import lax
from jax.experimental import pallas as pl
from jax.experimental.pallas import tpu as pltpu
from jax.sharding import PartitionSpec as P

LEN = 840
MESH = pl.DeviceIdType.MESH
BF16 = jnp.bfloat16
F32 = jnp.float32


def split(table):
    high = table.astype(BF16)
    low = (table - high.astype(np.float32)).astype(BF16)
    return high, low


def trig(bins, times):
    angle = 2.0 * np.pi * ((np.arange(times)[:, None] * np.arange(bins)[None, :]) % LEN) / LEN
    return np.cos(angle), np.sin(angle)


def spectrum_tables(groups, bins_dev, time_dev, probes):
    cosine, sine = trig(groups * bins_dev, groups * time_dev)
    scale = 1.0 / math.sqrt(groups * time_dev)
    both = np.stack([cosine, -sine], axis=0) * scale
    both = both.reshape(2, groups * time_dev, groups, bins_dev).transpose(2, 0, 3, 1)
    flat = np.repeat(both.reshape(groups, 2 * bins_dev, -1), probes, axis=-1).astype(np.float32)
    high, low = split(flat)
    return np.stack([high, low], axis=1)


def pick_tables(bins_dev, senses, keep):
    split_by = (bins_dev // 8, senses, 8, 2, keep)
    half, _, inner, part, _ = np.indices(split_by).reshape(len(split_by), -1)
    rows = np.arange(half.size)
    bins = half * 8 + inner
    first = np.zeros((half.size, 2 * bins_dev), np.float32)
    second = np.zeros_like(first)
    first[rows, part * bins_dev + bins] = 1.0
    second[rows, (1 - part) * bins_dev + bins] = np.where(part == 0, 1.0, -1.0)
    return np.stack([first, second]).astype(BF16)


def image_tables(groups, bins_dev, time_dev, keep):
    cosine, sine = trig(groups * bins_dev, groups * time_dev)
    both = np.stack([cosine, -sine], axis=2).reshape(groups, time_dev, groups, bins_dev, 2)
    both = both.transpose(2, 0, 1, 3, 4)
    full = np.einsum("ghtbc,qr->ghtqbcr", both, np.eye(keep)).astype(np.float32)
    flat = full.reshape(groups, groups, time_dev * keep, bins_dev * 2 * keep)
    high, low = split(flat)
    return np.concatenate([high, low, high], axis=-1)


def body(
    cfg,
    series_hbm,
    kernel_hbm,
    prior_hbm,
    scale_hbm,
    spec_hbm,
    img_hbm,
    pick_hbm,
    out_ref,
    kbuf,
    prior,
    scale,
    spec_tab,
    img_tab,
    pick,
    gathered,
    wide,
    spread,
    left_mat,
    weight,
    sbuf,
    rbuf,
    relay,
    joined,
    own,
    xsend,
    xrecv,
    halo_left,
    halo_right,
    small_sem,
    k_sem,
    g_send,
    g_recv,
    z_send,
    z_recv,
    relay_send,
    relay_recv,
    x_send,
    x_recv,
    hl_send,
    hl_recv,
    hr_send,
    hr_recv,
):
    groups, params, senses, chunks = cfg
    f = lax.axis_index("freq")
    k = lax.axis_index("param")
    s = lax.axis_index("sens")
    _, sens_dev, bins_dev, _ = kernel_hbm.shape
    halves = bins_dev // 8
    width = kbuf.shape[-1]
    block = wide.shape[2] // halves
    probes = block // 16
    keep = probes // senses
    edge = halo_left.shape[-1]

    def freq_peer(d):
        return lax.rem(f + d, groups)

    def sens_peer(d):
        return lax.rem(s + d, senses)

    small = [
        pltpu.make_async_copy(series_hbm, gathered.at[f], small_sem.at[0]),
        pltpu.make_async_copy(spec_hbm.at[f], spec_tab, small_sem.at[1]),
        pltpu.make_async_copy(prior_hbm, prior, small_sem.at[2]),
        pltpu.make_async_copy(scale_hbm, scale, small_sem.at[3]),
        pltpu.make_async_copy(img_hbm.at[f], img_tab, small_sem.at[4]),
        pltpu.make_async_copy(pick_hbm, pick, small_sem.at[5]),
    ]
    for copy in small:
        copy.start()
    loads = [
        [
            pltpu.make_async_copy(
                kernel_hbm.at[part, :, pl.ds(h * 8, 8), pl.ds(c * width, width)],
                kbuf.at[c, part, h],
                k_sem.at[c, part, h],
            )
            for h in range(halves)
            for part in range(2)
        ]
        for c in range(chunks)
    ]
    for group in loads:
        for copy in group:
            copy.start()

    barrier = pltpu.get_barrier_semaphore()
    for d in range(1, groups):
        pl.semaphore_signal(
            barrier, inc=1, device_id={"freq": freq_peer(d)}, device_id_type=MESH
        )
    for d in range(1, senses):
        pl.semaphore_signal(
            barrier, inc=1, device_id={"sens": sens_peer(d)}, device_id_type=MESH
        )
    has_left = k > 0
    has_right = k < params - 1

    @pl.when(has_left)
    def _():
        for d in range(groups):
            pl.semaphore_signal(
                barrier,
                inc=1,
                device_id={"freq": freq_peer(d), "param": k - 1},
                device_id_type=MESH,
            )

    @pl.when(has_right)
    def _():
        for d in range(groups):
            pl.semaphore_signal(
                barrier,
                inc=1,
                device_id={"freq": freq_peer(d), "param": k + 1},
                device_id_type=MESH,
            )

    small[0].wait()
    peers = groups + senses - 2
    beside = jnp.where(has_left, groups, 0) + jnp.where(has_right, groups, 0)
    pl.semaphore_wait(barrier, peers + beside)

    def series_copy(slot, target):
        return pltpu.make_async_remote_copy(
            src_ref=gathered.at[f],
            dst_ref=gathered.at[slot],
            send_sem=g_send.at[target],
            recv_sem=g_recv.at[slot],
            device_id={"freq": target},
            device_id_type=MESH,
        )

    for d in range(1, groups):
        series_copy(f, freq_peer(d)).start()
    for copy in small[1:]:
        copy.wait()
    probe_row = wide.shape[2]
    row = lax.broadcasted_iota(jnp.int32, (probe_row, wide.shape[3]), 0)
    lane = lax.broadcasted_iota(jnp.int32, (probe_row, wide.shape[3]), 1)
    probe = (row // (16 * keep)) % senses * keep + row % keep
    same = lane % probes == probe
    for v in range(2):
        for i in range(2):
            full = jnp.dot(pick[v], spec_tab[i], preferred_element_type=F32)
            wide[v, i] = jnp.where(same, full, 0.0).astype(BF16)
    row = lax.broadcasted_iota(jnp.int32, spread.shape, 0)
    lane = lax.broadcasted_iota(jnp.int32, spread.shape, 1)
    spread[...] = jnp.where(lane // 8 == row, 1.0, 0.0).astype(BF16)
    norm = 1.0 / math.sqrt(bins_dev * groups)
    row = lax.broadcasted_iota(jnp.int32, weight.shape[1:], 0)
    for h in range(halves):
        value = jnp.zeros(weight.shape[1:], F32)
        for b in range(8):
            value = jnp.where(row // (2 * keep) == b, prior[h * 8 + b] * norm, value)
        weight[h] = value

    for d in range(1, groups):
        series_copy(freq_peer(d), freq_peer(d)).wait_recv()
    rows = jnp.concatenate([gathered[g] for g in range(groups)], axis=0)
    row = lax.broadcasted_iota(jnp.int32, (block, spread.shape[1]), 0)
    lane = lax.broadcasted_iota(jnp.int32, (block, spread.shape[1]), 1)
    same = lane % 8 == row // (2 * keep) % 8
    for h in range(halves):
        for v in range(2):
            spec = jnp.dot(
                wide[v, 0, h * block : (h + 1) * block], rows, preferred_element_type=F32
            ) + jnp.dot(
                wide[v, 1, h * block : (h + 1) * block], rows, preferred_element_type=F32
            )
            full = jnp.dot(spec.astype(BF16), spread[...], preferred_element_type=F32)
            left_mat[v, h] = jnp.where(same, full, 0.0).astype(BF16)


    def z_copy(target, slot, c):
        return pltpu.make_async_remote_copy(
            src_ref=sbuf.at[target, c],
            dst_ref=rbuf.at[slot, c],
            send_sem=z_send.at[target, c],
            recv_sem=z_recv.at[slot, c],
            device_id={"sens": target},
            device_id_type=MESH,
        )

    paired = senses == 4
    if paired:
        pair = s + 1 - 2 * lax.rem(s, 2)
        across = senses - 1 - s
        other = senses - 1 - pair
        outer = jnp.logical_or(s == 0, s == senses - 1)
        inner = jnp.logical_not(outer)

        @pl.when(inner)
        def _():
            rbuf[other] = jnp.zeros(rbuf.shape[1:], BF16)

    def relay_copy(c):
        return pltpu.make_async_remote_copy(
            src_ref=sbuf.at[other, c],
            dst_ref=relay.at[c],
            send_sem=relay_send.at[c],
            recv_sem=relay_recv.at[c],
            device_id={"sens": pair},
            device_id_type=MESH,
        )

    def joined_copy(c):
        return pltpu.make_async_remote_copy(
            src_ref=joined.at[c],
            dst_ref=rbuf.at[s, c],
            send_sem=z_send.at[across, c],
            recv_sem=z_recv.at[s, c],
            device_id={"sens": across},
            device_id_type=MESH,
        )

    def send_sums(c):
        if not paired:
            for d in range(1, senses):
                z_copy(sens_peer(d), s, c).start()
            return

        @pl.when(outer)
        def _():
            relay_copy(c).start()
            z_copy(across, s, c).start()
            z_copy(pair, s, c).start()

        @pl.when(inner)
        def _():
            z_copy(other, s, c).start()
            z_copy(pair, s, c).start()

    def pass_on(c):
        if not paired or c >= chunks:
            return

        @pl.when(inner)
        def _():
            relay_copy(c).wait_recv()
            both = sbuf[across, c].astype(F32) + relay[c].astype(F32)
            joined[c] = both.astype(BF16)
            joined_copy(c).start()

    def collect(c):
        total = sbuf[s, c].astype(F32)
        if not paired:
            for d in range(1, senses):
                z_copy(sens_peer(d), sens_peer(d), c).wait_recv()
                total = total + rbuf[sens_peer(d), c].astype(F32)
            return total
        z_copy(pair, pair, c).wait_recv()

        @pl.when(outer)
        def _():
            z_copy(other, other, c).wait_recv()

        z_copy(across, across, c).wait_recv()
        for slot in (pair, other, across):
            total = total + rbuf[slot, c].astype(F32)
        return total

    def drain(c):
        if not paired:
            for d in range(1, senses):
                z_copy(sens_peer(d), s, c).wait_send()
            return

        @pl.when(outer)
        def _():
            relay_copy(c).wait_send()
            z_copy(across, s, c).wait_send()
            z_copy(pair, s, c).wait_send()

        @pl.when(inner)
        def _():
            z_copy(other, s, c).wait_send()
            z_copy(pair, s, c).wait_send()
            joined_copy(c).wait_send()

    for c in range(chunks):
        for h in range(halves):
            total = jnp.zeros((block, width), F32)
            for part in range(2):
                loads[c][h * 2 + part].wait()
                right_mat = kbuf.at[c, part, h].reshape(sens_dev * 8, width)[...]
                total = total + jnp.dot(
                    left_mat[part, h], right_mat, preferred_element_type=F32
                )
            each = block // senses
            for j in range(senses):
                piece = total[j * each : (j + 1) * each] * weight[h]
                sbuf[j, c, h * each : (h + 1) * each, :] = piece.astype(BF16)
        send_sums(c)

    def x_copy(target, slot, c):
        return pltpu.make_async_remote_copy(
            src_ref=xsend.at[target, c],
            dst_ref=xrecv.at[slot, c],
            send_sem=x_send.at[target, c],
            recv_sem=x_recv.at[slot, c],
            device_id={"freq": target},
            device_id_type=MESH,
        )

    def to_left(target, slot):
        return pltpu.make_async_remote_copy(
            src_ref=xsend.at[target, 0, :, pl.ds(0, edge)],
            dst_ref=halo_right.at[slot],
            send_sem=hl_send.at[target],
            recv_sem=hr_recv.at[slot],
            device_id={"freq": target, "param": jnp.maximum(k - 1, 0)},
            device_id_type=MESH,
        )

    def to_right(target, slot):
        return pltpu.make_async_remote_copy(
            src_ref=xsend.at[target, chunks - 1, :, pl.ds(width - edge, edge)],
            dst_ref=halo_left.at[slot],
            send_sem=hr_send.at[target],
            recv_sem=hl_recv.at[slot],
            device_id={"freq": target, "param": jnp.minimum(k + 1, params - 1)},
            device_id_type=MESH,
        )

    pass_on(0)
    for c in range(chunks):
        pass_on(c + 1)
        total = collect(c)
        high = total.astype(BF16)
        low = (total - high.astype(F32)).astype(BF16)
        stacked = jnp.concatenate([high, high, low], axis=0)
        lanes = scale[:, c * width : (c + 1) * width]
        for d in list(range(1, groups)) + [0]:
            g = freq_peer(d)
            image = jnp.dot(img_tab[g], stacked, preferred_element_type=F32) * lanes
            if d == 0:
                own[c] = image
                if c == 0 or c == chunks - 1:
                    xsend[g, c] = image.astype(BF16)
            else:
                xsend[g, c] = image.astype(BF16)
                x_copy(g, f, c).start()
        if c == 0:

            @pl.when(has_left)
            def _():
                for d in range(groups):
                    to_left(freq_peer(d), f).start()

        if c == chunks - 1:

            @pl.when(has_right)
            def _():
                for d in range(groups):
                    to_right(freq_peer(d), f).start()

    for c in range(chunks):
        image = own[c]
        for d in range(1, groups):
            g = freq_peer(d)
            x_copy(g, g, c).wait_recv()
            image = image + xrecv[g, c].astype(F32)
        own[c] = image


    @pl.when(has_left)
    def _():
        for d in range(groups):
            to_right(freq_peer(d), freq_peer(d)).wait_recv()

    @pl.when(jnp.logical_not(has_left))
    def _():
        halo_left[...] = jnp.zeros_like(halo_left)

    @pl.when(has_right)
    def _():
        for d in range(groups):
            to_left(freq_peer(d), freq_peer(d)).wait_recv()

    @pl.when(jnp.logical_not(has_right))
    def _():
        halo_right[...] = jnp.zeros_like(halo_right)

    left = halo_left[0].astype(F32)
    right = halo_right[0].astype(F32)
    for g in range(1, groups):
        left = left + halo_left[g].astype(F32)
        right = right + halo_right[g].astype(F32)
    for c in range(chunks):
        mid = own[c]
        before = own[c - 1][:, width - 1 :] if c > 0 else left[:, edge - 1 :]
        after = own[c + 1][:, :1] if c < chunks - 1 else right[:, :1]
        lower = jnp.concatenate([before, mid[:, :-1]], axis=1)
        upper = jnp.concatenate([mid[:, 1:], after], axis=1)
        lanes = scale[:, c * width : (c + 1) * width]
        out_ref[:, c * width : (c + 1) * width] = lanes * (0.5 * mid + 0.25 * (lower + upper))

    for d in range(1, groups):
        series_copy(f, freq_peer(d)).wait_send()
        for c in range(chunks):
            x_copy(freq_peer(d), f, c).wait_send()
    for c in range(chunks):
        drain(c)

    @pl.when(has_left)
    def _():
        for d in range(groups):
            to_left(freq_peer(d), f).wait_send()

    @pl.when(has_right)
    def _():
        for d in range(groups):
            to_right(freq_peer(d), f).wait_send()


def local(mesh_shape, series, kernel, prior_spectrum, prior_scale):
    groups, params, senses = (mesh_shape[n] for n in ("freq", "param", "sens"))
    probes, sens_dev, time_dev = series.shape
    _, bins_dev, _, cols = kernel.shape
    keep = probes // senses
    chunks = 4
    width = cols // chunks
    edge = min(128, width)
    rows = time_dev * keep
    depth = bins_dev * 2 * keep
    halves = bins_dev // 8
    block = 16 * probes
    spec_tab = spectrum_tables(groups, bins_dev, time_dev, probes)
    pick_tab = pick_tables(bins_dev, senses, keep)
    img_tab = image_tables(groups, bins_dev, time_dev, keep)
    dma = pltpu.SemaphoreType.DMA
    out = pl.pallas_call(
        functools.partial(body, (groups, params, senses, chunks)),
        out_shape=jax.ShapeDtypeStruct((rows, cols), F32),
        in_specs=[pl.BlockSpec(memory_space=pltpu.HBM)] * 7,
        out_specs=pl.BlockSpec(memory_space=pltpu.VMEM),
        scratch_shapes=[
            pltpu.VMEM((chunks, 2, halves, sens_dev, 8, width), BF16),
            pltpu.SMEM((bins_dev,), F32),
            pltpu.VMEM((1, cols), F32),
            pltpu.VMEM(spec_tab.shape[1:], BF16),
            pltpu.VMEM(img_tab.shape[1:], BF16),
            pltpu.VMEM(pick_tab.shape, BF16),
            pltpu.VMEM((groups, time_dev * probes, sens_dev), BF16),
            pltpu.VMEM((2, 2, halves * block, groups * time_dev * probes), BF16),
            pltpu.VMEM((sens_dev, sens_dev * 8), BF16),
            pltpu.VMEM((2, halves, block, sens_dev * 8), BF16),
            pltpu.VMEM((halves, block // senses, width), F32),
            pltpu.VMEM((senses, chunks, depth, width), BF16),
            pltpu.VMEM((senses, chunks, depth, width), BF16),
            pltpu.VMEM((chunks, depth, width), BF16),
            pltpu.VMEM((chunks, depth, width), BF16),
            pltpu.VMEM((chunks, rows, width), F32),
            pltpu.VMEM((groups, chunks, rows, width), BF16),
            pltpu.VMEM((groups, chunks, rows, width), BF16),
            pltpu.VMEM((groups, rows, edge), BF16),
            pltpu.VMEM((groups, rows, edge), BF16),
            dma((6,)),
            dma((chunks, 2, halves)),
            dma((groups,)),
            dma((groups,)),
            dma((senses, chunks)),
            dma((senses, chunks)),
            dma((chunks,)),
            dma((chunks,)),
            dma((groups, chunks)),
            dma((groups, chunks)),
            dma((groups,)),
            dma((groups,)),
            dma((groups,)),
            dma((groups,)),
        ],
        compiler_params=pltpu.CompilerParams(
            collective_id=0, has_side_effects=True, vmem_limit_bytes=60 * 1024 * 1024
        ),
    )(
        series.transpose(2, 0, 1).reshape(time_dev * probes, sens_dev),
        kernel.transpose(0, 2, 1, 3),
        prior_spectrum,
        prior_scale.reshape(1, cols),
        jnp.asarray(spec_tab),
        jnp.asarray(img_tab),
        jnp.asarray(pick_tab),
    )
    return out.reshape(time_dev, keep, cols)


def solution(mesh):
    placed = (P(None, "sens", "freq"), P(None, "freq", "sens", "param"), P("freq"), P("param"))
    return jax.shard_map(
        functools.partial(local, dict(mesh.shape)),
        mesh=mesh,
        in_specs=placed,
        out_specs=P("freq", "sens", "param"),
        check_vma=False,
    )
```

profile of v0, /device:TPU:0, one launch (start us, length us, event | category | flops | bytes accessed | tf_op | source)
XLA Modules:
  0.0 29.6 jit_solution(16611527716215723464)
XLA Ops:
  0.0 27.9 %shard_map.73 = f32[52,1024]{1,0:T(8,128)} custom-call(bf16[208,150]{1,0:T(8,128)(2,1)} %bitcast.6, bf16[2,150,16,1024]{3,2,1,0:T(8,128)(2,1)} %bitcast.5, f32[16]{0:T(128)} %prior_hbm.1, f32[1,1024]{1,0:T(1,128)} %bitcast.7, bf16[2,2,32,416]{3,2,1,0:T(8,128)(2,1)} %constant.6.clone.spec_hbm, bf16[2,2,52,192]{3,2,1,0:T(8,128)(2,1)} %constant.7.clone.img_hbm, ...), custom_call_target="tpu_custom_call" | custom-call | tf_op jit(solution)/shard_map/pallas_call | solution.py:496
  27.9 1.7 %reshape.11 = f32[26,2,1024]{2,1,0:T(2,128)} reshape(f32[52,1024]{1,0:T(8,128)} %shard_map.73) | data formatting | bytes 425984 | tf_op jit(solution)/shard_map/reshape | solution.py:549
where the time goes:
time: 29.7 us; the launch traced here: 29.6 us
  Pallas kernels  27.9 us (94%)
  local copies, waits for them, and re-layouts  1.74 us (6%)
    pallas_call x1, Pallas kernels, local(): pl.pallas_call(functools.partial(body, (groups, params, senses, chunks)),...  27.9 us
    reshape x1, local copies, waits for them, and re-layouts, local(): return out.reshape(time_dev, keep, cols)  1.74 us

commit v1 on v0

v1 whole, which is shorter than its diff:
```python
import functools
import math

import jax
import jax.numpy as jnp
import numpy as np
from jax import lax
from jax.experimental import pallas as pl
from jax.experimental.pallas import tpu as pltpu
from jax.sharding import PartitionSpec as P

LEN = 840
MESH = pl.DeviceIdType.MESH
BF16 = jnp.bfloat16
F32 = jnp.float32
RESIDUAL = 2.0**-26
STEP = 256


def split(table):
    table = table.astype(np.float32)
    high = table.astype(BF16)
    low = (table - high.astype(np.float32)).astype(BF16)
    return high, low


def phases(groups, bins_dev, time_dev):
    bins, times = groups * bins_dev, groups * time_dev
    angle = 2.0 * np.pi * ((np.arange(times)[:, None] * np.arange(bins)[None, :]) % LEN) / LEN
    both = np.stack([np.cos(angle), -np.sin(angle)], axis=1)
    both = both.reshape(times, 2, groups, bins_dev).transpose(2, 0, 1, 3)
    return both.reshape(groups, times, 2 * bins_dev)


def factor(table, multiple):
    left, size, right = np.linalg.svd(table, full_matrices=False)
    rank = size.size
    for r in range(1, size.size):
        if np.abs(table - (left[:, :r] * size[:r]) @ right[:r]).max() < RESIDUAL:
            rank = r
            break
    rank = min(-(-rank // multiple) * multiple, size.size)
    return left * size, right, rank


def with_probes(table, probes):
    full = np.einsum("...ij,qr->...iqjr", table, np.eye(probes))
    lead = table.shape[:-2]
    return full.reshape(lead + (table.shape[-2] * probes, table.shape[-1] * probes))


def series_tables(groups, bins_dev, time_dev, probes):
    comps = phases(groups, bins_dev, time_dev) / math.sqrt(groups * time_dev)
    blocks = comps.reshape(groups, groups, time_dev, 2 * bins_dev).transpose(0, 1, 3, 2)
    parts = [factor(block.reshape(-1, time_dev), 2) for block in blocks]
    rank = max(part[2] for part in parts)
    short = np.stack([right[:rank] for _, right, _ in parts])
    long = np.stack([left[:, :rank] for left, _, _ in parts])
    long = long.reshape(groups, groups, 2 * bins_dev, rank)
    own = np.stack([blocks[g, g] for g in range(groups)])
    tables = [np.stack(split(with_probes(t, probes)), axis=-3) for t in (short, long, own)]
    return tables, rank


def image_tables(groups, bins_dev, time_dev, keep):
    comps = phases(groups, bins_dev, time_dev)
    parts = [factor(comp, 8) for comp in comps]
    rank = max(part[2] for part in parts)
    outer = np.stack([left[:, :rank] for left, _, _ in parts])
    outer = outer.reshape(groups, groups, time_dev, rank).transpose(1, 2, 0, 3)
    outer = outer.reshape(groups, time_dev, groups * rank)
    full = np.einsum("gtj,qr->gtqjr", outer, np.eye(keep))
    full = full.reshape(groups, time_dev * keep, groups * rank * keep)
    image = np.concatenate(split(full), axis=-1)
    inner = np.stack([right[:rank] for _, right, _ in parts])
    inner = inner.reshape(groups, rank, 2, bins_dev).transpose(0, 2, 1, 3)
    inner = np.repeat(inner, keep, axis=2)
    return image, np.tile(inner, (1, 1, 1, STEP // bins_dev)).astype(np.float32), rank


def body(
    cfg,
    series_hbm,
    kernel_hbm,
    prior_hbm,
    scale_hbm,
    short_hbm,
    long_hbm,
    own_hbm,
    img_hbm,
    inner_hbm,
    out_ref,
    kbuf,
    rows,
    prior,
    scale,
    short,
    long,
    own,
    img_tab,
    inner,
    squeezed,
    arrived,
    spread,
    ebuf,
    left_mat,
    sbuf,
    rbuf,
    relay,
    joined,
    gath,
    edges,
    halo_left,
    halo_right,
    small_sem,
    k_sem,
    g_send,
    g_recv,
    z_send,
    z_recv,
    relay_send,
    relay_recv,
    x_send,
    x_recv,
    hl_send,
    hl_recv,
    hr_send,
    hr_recv,
):
    groups, params, senses, chunks, bins_dev, probes = cfg
    f = lax.axis_index("freq")
    k = lax.axis_index("param")
    s = lax.axis_index("sens")
    depth = kernel_hbm.shape[1]
    width = kbuf.shape[-1]
    keep = probes // senses
    edge = halo_left.shape[-1]
    each = gath.shape[2]
    order = [0, chunks - 1] + list(range(1, chunks - 1)) if chunks > 1 else [0]

    def freq_peer(d):
        return lax.rem(f + d, groups)

    def sens_peer(d):
        return lax.rem(s + d, senses)

    small = [
        pltpu.make_async_copy(series_hbm, rows, small_sem.at[0]),
        pltpu.make_async_copy(short_hbm, short, small_sem.at[1]),
        pltpu.make_async_copy(own_hbm.at[f], own, small_sem.at[2]),
        pltpu.make_async_copy(long_hbm.at[f], long, small_sem.at[3]),
        pltpu.make_async_copy(prior_hbm, prior, small_sem.at[4]),
        pltpu.make_async_copy(inner_hbm.at[f], inner, small_sem.at[5]),
        pltpu.make_async_copy(scale_hbm, scale, small_sem.at[6]),
        pltpu.make_async_copy(img_hbm.at[f], img_tab, small_sem.at[7]),
    ]
    for copy in small:
        copy.start()

    barrier = pltpu.get_barrier_semaphore()
    for d in range(1, groups):
        pl.semaphore_signal(
            barrier, inc=1, device_id={"freq": freq_peer(d)}, device_id_type=MESH
        )
    for d in range(1, senses):
        pl.semaphore_signal(
            barrier, inc=1, device_id={"sens": sens_peer(d)}, device_id_type=MESH
        )
    has_left = k > 0
    has_right = k < params - 1

    @pl.when(has_left)
    def _():
        for d in range(groups):
            pl.semaphore_signal(
                barrier,
                inc=1,
                device_id={"freq": freq_peer(d), "param": k - 1},
                device_id_type=MESH,
            )

    @pl.when(has_right)
    def _():
        for d in range(groups):
            pl.semaphore_signal(
                barrier,
                inc=1,
                device_id={"freq": freq_peer(d), "param": k + 1},
                device_id_type=MESH,
            )

    small[0].wait()
    small[1].wait()
    loads = [
        [
            pltpu.make_async_copy(
                kernel_hbm.at[part, :, pl.ds(c * width, width)],
                kbuf.at[c, part],
                k_sem.at[c, part],
            )
            for part in range(2)
        ]
        for c in range(chunks)
    ]
    for c in order:
        for copy in loads[c]:
            copy.start()

    series = rows[...]
    for d in range(1, groups):
        g = freq_peer(d)
        squeezed[g] = (
            jnp.dot(short[g, 0], series, preferred_element_type=F32)
            + jnp.dot(short[g, 1], series, preferred_element_type=F32)
        ).astype(BF16)

    peers = groups + senses - 2
    beside = jnp.where(has_left, groups, 0) + jnp.where(has_right, groups, 0)
    pl.semaphore_wait(barrier, peers + beside)

    def series_copy(target, slot):
        return pltpu.make_async_remote_copy(
            src_ref=squeezed.at[target],
            dst_ref=arrived.at[slot],
            send_sem=g_send.at[target],
            recv_sem=g_recv.at[slot],
            device_id={"freq": target},
            device_id_type=MESH,
        )

    for d in range(1, groups):
        series_copy(freq_peer(d), f).start()
    for copy in small[2:]:
        copy.wait()
    row = lax.broadcasted_iota(jnp.int32, spread.shape, 0)
    lane = lax.broadcasted_iota(jnp.int32, spread.shape, 1)
    spread[...] = jnp.where(lane // bins_dev == row, 1.0, 0.0).astype(BF16)
    norm = 1.0 / math.sqrt(bins_dev * groups)
    lane = lax.broadcasted_iota(jnp.int32, (8, STEP), 1) % bins_dev
    value = jnp.zeros((8, STEP), F32)
    for b in range(bins_dev):
        value = jnp.where(lane == b, prior[b] * norm, value)
    inner[...] = inner[...] * value[:1]
    spec = jnp.dot(own[0], series, preferred_element_type=F32) + jnp.dot(
        own[1], series, preferred_element_type=F32
    )
    for d in range(1, groups):
        g = freq_peer(d)
        series_copy(g, g).wait_recv()
        came = arrived[g]
        spec = (
            spec
            + jnp.dot(long[g, 0], came, preferred_element_type=F32)
            + jnp.dot(long[g, 1], came, preferred_element_type=F32)
        )
    spec = spec.astype(BF16)
    odd = lax.broadcasted_iota(jnp.int32, (8, STEP), 0) % keep
    comp = bins_dev * probes
    for n in range(spread.shape[1] // STEP):
        cut = slice(n * STEP, (n + 1) * STEP)
        full = jnp.dot(spec, spread[:, cut], preferred_element_type=F32)
        for q in range(2):
            chosen = full[q * comp : q * comp + probes]
            for b in range(1, bins_dev):
                at = q * comp + b * probes
                chosen = jnp.where(lane[:probes] == b, full[at : at + probes], chosen)
            ebuf[q, :, cut] = chosen
        for j in range(senses):
            pair_of = []
            for q in range(2):
                e = jnp.broadcast_to(ebuf[q, j * keep : j * keep + 1, cut], (8, STEP))
                for r in range(1, keep):
                    at = j * keep + r
                    e = jnp.where(odd == r, ebuf[q, at : at + 1, cut], e)
                pair_of.append(jnp.concatenate([e] * (each // 8), axis=0))
            re, im = pair_of
            left_mat[0, j * each : (j + 1) * each, cut] = (inner[0] * re + inner[1] * im).astype(BF16)
            left_mat[1, j * each : (j + 1) * each, cut] = (inner[0] * im - inner[1] * re).astype(BF16)

    def z_copy(target, slot, c):
        return pltpu.make_async_remote_copy(
            src_ref=sbuf.at[target, c],
            dst_ref=rbuf.at[slot, c],
            send_sem=z_send.at[target, c],
            recv_sem=z_recv.at[slot, c],
            device_id={"sens": target},
            device_id_type=MESH,
        )

    paired = senses == 4
    if paired:
        pair = s + 1 - 2 * lax.rem(s, 2)
        across = senses - 1 - s
        other = senses - 1 - pair
        outer = jnp.logical_or(s == 0, s == senses - 1)
        within = jnp.logical_not(outer)

        @pl.when(within)
        def _():
            rbuf[other] = jnp.zeros(rbuf.shape[1:], BF16)

    def relay_copy(c):
        return pltpu.make_async_remote_copy(
            src_ref=sbuf.at[other, c],
            dst_ref=relay.at[c],
            send_sem=relay_send.at[c],
            recv_sem=relay_recv.at[c],
            device_id={"sens": pair},
            device_id_type=MESH,
        )

    def joined_copy(c):
        return pltpu.make_async_remote_copy(
            src_ref=joined.at[c],
            dst_ref=rbuf.at[s, c],
            send_sem=z_send.at[across, c],
            recv_sem=z_recv.at[s, c],
            device_id={"sens": across},
            device_id_type=MESH,
        )

    def send_sums(c):
        if not paired:
            for d in range(1, senses):
                z_copy(sens_peer(d), s, c).start()
            return

        @pl.when(outer)
        def _():
            relay_copy(c).start()
            z_copy(across, s, c).start()
            z_copy(pair, s, c).start()

        @pl.when(within)
        def _():
            z_copy(other, s, c).start()
            z_copy(pair, s, c).start()

    def pass_on(c):
        if not paired:
            return

        @pl.when(within)
        def _():
            relay_copy(c).wait_recv()
            both = sbuf[across, c].astype(F32) + relay[c].astype(F32)
            joined[c] = both.astype(BF16)
            joined_copy(c).start()

    def collect(c):
        total = sbuf[s, c].astype(F32)
        if not paired:
            for d in range(1, senses):
                z_copy(sens_peer(d), sens_peer(d), c).wait_recv()
                total = total + rbuf[sens_peer(d), c].astype(F32)
            return total
        z_copy(pair, pair, c).wait_recv()

        @pl.when(outer)
        def _():
            z_copy(other, other, c).wait_recv()

        z_copy(across, across, c).wait_recv()
        for slot in (pair, other, across):
            total = total + rbuf[slot, c].astype(F32)
        return total

    def drain(c):
        if not paired:
            for d in range(1, senses):
                z_copy(sens_peer(d), s, c).wait_send()
            return

        @pl.when(outer)
        def _():
            relay_copy(c).wait_send()
            z_copy(across, s, c).wait_send()
            z_copy(pair, s, c).wait_send()

        @pl.when(within)
        def _():
            z_copy(other, s, c).wait_send()
            z_copy(pair, s, c).wait_send()
            joined_copy(c).wait_send()

    for c in order:
        total = jnp.zeros((senses * each, width), F32)
        for part in range(2):
            loads[c][part].wait()
            total = total + jnp.dot(
                left_mat[part, :, :depth], kbuf[c, part], preferred_element_type=F32
            )
        for j in range(senses):
            sbuf[j, c] = total[j * each : (j + 1) * each].astype(BF16)
        send_sums(c)

    def x_copy(target, slot, c):
        return pltpu.make_async_remote_copy(
            src_ref=gath.at[f, c],
            dst_ref=gath.at[slot, c],
            send_sem=x_send.at[target, c],
            recv_sem=x_recv.at[slot, c],
            device_id={"freq": target},
            device_id_type=MESH,
        )

    def to_left(target, slot):
        return pltpu.make_async_remote_copy(
            src_ref=edges.at[0],
            dst_ref=halo_right.at[slot],
            send_sem=hl_send.at[target],
            recv_sem=hr_recv.at[slot],
            device_id={"freq": target, "param": jnp.maximum(k - 1, 0)},
            device_id_type=MESH,
        )

    def to_right(target, slot):
        return pltpu.make_async_remote_copy(
            src_ref=edges.at[1],
            dst_ref=halo_left.at[slot],
            send_sem=hr_send.at[target],
            recv_sem=hl_recv.at[slot],
            device_id={"freq": target, "param": jnp.minimum(k + 1, params - 1)},
            device_id_type=MESH,
        )

    cols = chunks * width
    pass_on(order[0])
    for i, c in enumerate(order):
        if i + 1 < chunks:
            pass_on(order[i + 1])
        total = collect(c)
        gath[f, c] = total.astype(BF16)
        for d in range(1, groups):
            x_copy(freq_peer(d), f, c).start()
        if c == 0:
            edges[0] = (total[:, :edge] * scale[:, :edge]).astype(BF16)

            @pl.when(has_left)
            def _():
                for d in range(groups):
                    to_left(freq_peer(d), f).start()

        if c == chunks - 1:
            edges[1] = (total[:, width - edge :] * scale[:, cols - edge :]).astype(BF16)

            @pl.when(has_right)
            def _():
                for d in range(groups):
                    to_right(freq_peer(d), f).start()

    @pl.when(has_left)
    def _():
        for d in range(groups):
            to_right(freq_peer(d), freq_peer(d)).wait_recv()

    @pl.when(jnp.logical_not(has_left))
    def _():
        halo_left[...] = jnp.zeros_like(halo_left)

    @pl.when(has_right)
    def _():
        for d in range(groups):
            to_left(freq_peer(d), freq_peer(d)).wait_recv()

    @pl.when(jnp.logical_not(has_right))
    def _():
        halo_right[...] = jnp.zeros_like(halo_right)

    def image_of(stack):
        return jnp.dot(
            img_tab[...], jnp.concatenate(stack + stack, axis=0), preferred_element_type=F32
        )

    left = image_of([halo_left[g] for g in range(groups)])
    right = image_of([halo_right[g] for g in range(groups)])
    scaled = [None] * chunks
    for c in order:
        for d in range(1, groups):
            g = freq_peer(d)
            x_copy(g, g, c).wait_recv()
        lanes = scale[:, c * width : (c + 1) * width]
        scaled[c] = image_of([gath[g, c] for g in range(groups)]) * lanes

    for c in range(chunks):
        mid = scaled[c]
        before = scaled[c - 1][:, width - 1 :] if c > 0 else left[:, edge - 1 :]
        after = scaled[c + 1][:, :1] if c < chunks - 1 else right[:, :1]
        lower = jnp.concatenate([before, mid[:, :-1]], axis=1)
        upper = jnp.concatenate([mid[:, 1:], after], axis=1)
        lanes = scale[:, c * width : (c + 1) * width]
        out_ref[:, c * width : (c + 1) * width] = lanes * (0.5 * mid + 0.25 * (lower + upper))

    for d in range(1, groups):
        series_copy(freq_peer(d), f).wait_send()
        for c in range(chunks):
            x_copy(freq_peer(d), f, c).wait_send()
    for c in range(chunks):
        drain(c)

    @pl.when(has_left)
    def _():
        for d in range(groups):
            to_left(freq_peer(d), f).wait_send()

    @pl.when(has_right)
    def _():
        for d in range(groups):
            to_right(freq_peer(d), f).wait_send()


def local(mesh_shape, series, kernel, prior_spectrum, prior_scale):
    groups, params, senses = (mesh_shape[n] for n in ("freq", "param", "sens"))
    probes, sens_dev, time_dev = series.shape
    _, bins_dev, _, cols = kernel.shape
    keep = probes // senses
    chunks = 4
    width = cols // chunks
    edge = min(128, width)
    rows = time_dev * keep
    depth = sens_dev * bins_dev
    steps = -(-depth // STEP) * STEP
    (short, long, own), squeeze = series_tables(groups, bins_dev, time_dev, probes)
    img_tab, inner, rank = image_tables(groups, bins_dev, time_dev, keep)
    each = rank * keep
    dma = pltpu.SemaphoreType.DMA
    out = pl.pallas_call(
        functools.partial(body, (groups, params, senses, chunks, bins_dev, probes)),
        out_shape=jax.ShapeDtypeStruct((rows, cols), F32),
        in_specs=[pl.BlockSpec(memory_space=pltpu.HBM)] * 9,
        out_specs=pl.BlockSpec(memory_space=pltpu.VMEM),
        scratch_shapes=[
            pltpu.VMEM((chunks, 2, depth, width), BF16),
            pltpu.VMEM((time_dev * probes, sens_dev), BF16),
            pltpu.SMEM((bins_dev,), F32),
            pltpu.VMEM((1, cols), F32),
            pltpu.VMEM(short.shape, BF16),
            pltpu.VMEM(long.shape[1:], BF16),
            pltpu.VMEM(own.shape[1:], BF16),
            pltpu.VMEM(img_tab.shape[1:], BF16),
            pltpu.VMEM(inner.shape[1:], F32),
            pltpu.VMEM((groups, squeeze * probes, sens_dev), BF16),
            pltpu.VMEM((groups, squeeze * probes, sens_dev), BF16),
            pltpu.VMEM((sens_dev, steps), BF16),
            pltpu.VMEM((2, probes, steps), F32),
            pltpu.VMEM((2, senses * each, steps), BF16),
            pltpu.VMEM((senses, chunks, each, width), BF16),
            pltpu.VMEM((senses, chunks, each, width), BF16),
            pltpu.VMEM((chunks, each, width), BF16),
            pltpu.VMEM((chunks, each, width), BF16),
            pltpu.VMEM((groups, chunks, each, width), BF16),
            pltpu.VMEM((2, each, edge), BF16),
            pltpu.VMEM((groups, each, edge), BF16),
            pltpu.VMEM((groups, each, edge), BF16),
            dma((8,)),
            dma((chunks, 2)),
            dma((groups,)),
            dma((groups,)),
            dma((senses, chunks)),
            dma((senses, chunks)),
            dma((chunks,)),
            dma((chunks,)),
            dma((groups, chunks)),
            dma((groups, chunks)),
            dma((groups,)),
            dma((groups,)),
            dma((groups,)),
            dma((groups,)),
        ],
        compiler_params=pltpu.CompilerParams(
            collective_id=0, has_side_effects=True, vmem_limit_bytes=60 * 1024 * 1024
        ),
    )(
        series.transpose(2, 0, 1).reshape(time_dev * probes, sens_dev),
        kernel.transpose(0, 2, 1, 3).reshape(2, depth, cols),
        prior_spectrum,
        prior_scale.reshape(1, cols),
        jnp.asarray(short),
        jnp.asarray(long),
        jnp.asarray(own),
        jnp.asarray(img_tab),
        jnp.asarray(inner),
    )
    return out.reshape(time_dev, keep, cols)


def solution(mesh):
    placed = (P(None, "sens", "freq"), P(None, "freq", "sens", "param"), P("freq"), P("param"))
    return jax.shard_map(
        functools.partial(local, dict(mesh.shape)),
        mesh=mesh,
        in_specs=placed,
        out_specs=P("freq", "sens", "param"),
        check_vma=False,
    )
```

time: 29.7 us -> 23.7 us (0.80)
  the two profiles are of different devices: /device:TPU:0 before, /device:TPU:8 now
where the time goes in v1:
time: 23.7 us; the launch traced here: 23.6 us
  Pallas kernels  21.8 us (92%)
  local copies, waits for them, and re-layouts  1.74 us (7%)
    pallas_call x1, Pallas kernels, local(): pl.pallas_call(functools.partial(body, (groups, params, senses, chunks, b...  21.8 us
    reshape x1, local copies, waits for them, and re-layouts, local(): return out.reshape(time_dev, keep, cols)  1.74 us

profile of v1, /device:TPU:8, one launch (start us, length us, event | category | flops | bytes accessed | tf_op | source)
XLA Modules:
  0.0 23.6 jit_solution(7844179089594719450)
XLA Ops:
  0.0 21.8 %shard_map.91 = f32[52,1024]{1,0:T(8,128)} custom-call(bf16[208,150]{1,0:T(8,128)(2,1)} %bitcast.8, bf16[2,2400,1024]{2,1,0:T(8,128)(2,1)} %bitcast.7, f32[16]{0:T(128)} %prior_hbm.1, f32[1,1024]{1,0:T(1,128)} %bitcast.9, bf16[2,2,80,208]{3,2,1,0:T(8,128)(2,1)} %constant.10.clone.short_hbm, bf16[2,2,2,256,80]{4,3,2,1,0:T(8,128)(2,1)} %constant.11.clone.long_hbm, ...), custom_call_target="tpu_custom_call" | custom-call | tf_op jit(solution)/shard_map/pallas_call | solution.py:527
  21.8 1.7 %reshape.15 = f32[26,2,1024]{2,1,0:T(2,128)} reshape(f32[52,1024]{1,0:T(8,128)} %shard_map.91) | data formatting | bytes 425984 | tf_op jit(solution)/shard_map/reshape | solution.py:584

commit v2 on v1

v2 whole, which is shorter than its diff:
```python
import functools
import math

import jax
import jax.numpy as jnp
import numpy as np
from jax import lax
from jax.experimental import pallas as pl
from jax.experimental.pallas import tpu as pltpu
from jax.sharding import PartitionSpec as P

LEN = 840
MESH = pl.DeviceIdType.MESH
BF16 = jnp.bfloat16
F32 = jnp.float32
RESIDUAL = 2.0**-26
STEP = 256
LANES = 128


def split(table):
    table = table.astype(np.float32)
    high = table.astype(BF16)
    low = (table - high.astype(np.float32)).astype(BF16)
    return high, low


def phases(groups, bins_dev, time_dev):
    bins, times = groups * bins_dev, groups * time_dev
    angle = 2.0 * np.pi * ((np.arange(times)[:, None] * np.arange(bins)[None, :]) % LEN) / LEN
    both = np.stack([np.cos(angle), -np.sin(angle)], axis=1)
    both = both.reshape(times, 2, groups, bins_dev).transpose(2, 0, 1, 3)
    return both.reshape(groups, times, 2 * bins_dev)


def factor(table, multiple):
    left, size, right = np.linalg.svd(table, full_matrices=False)
    rank = size.size
    for r in range(1, size.size):
        if np.abs(table - (left[:, :r] * size[:r]) @ right[:r]).max() < RESIDUAL:
            rank = r
            break
    rank = min(-(-rank // multiple) * multiple, size.size)
    return left * size, right, rank


def with_probes(table, probes):
    full = np.einsum("...ij,qr->...iqjr", table, np.eye(probes))
    lead = table.shape[:-2]
    return full.reshape(lead + (table.shape[-2] * probes, table.shape[-1] * probes))


def series_tables(groups, bins_dev, time_dev, probes):
    comps = phases(groups, bins_dev, time_dev) / math.sqrt(groups * time_dev)
    blocks = comps.reshape(groups, groups, time_dev, 2 * bins_dev).transpose(0, 1, 3, 2)
    parts = [factor(block.reshape(-1, time_dev), 2) for block in blocks]
    rank = max(part[2] for part in parts)
    short = np.stack([right[:rank] for _, right, _ in parts])
    short = np.stack(split(with_probes(short, probes)), axis=1)
    long = np.stack([left[:, :rank] for left, _, _ in parts])
    long = long.reshape(groups, groups, 2, bins_dev, rank).transpose(0, 1, 2, 4, 3)
    long = np.stack([np.roll(long[g], -g, axis=0) for g in range(groups)])
    return short, long.reshape(groups, -1, bins_dev), rank


def image_tables(groups, bins_dev, time_dev, keep):
    comps = phases(groups, bins_dev, time_dev)
    parts = [factor(comp, 8) for comp in comps]
    rank = max(part[2] for part in parts)
    outer = np.stack([left[:, :rank] for left, _, _ in parts])
    outer = outer.reshape(groups, groups, time_dev, rank).transpose(1, 2, 0, 3)
    full = np.einsum("gthj,qr->gtqhjr", outer, np.eye(keep))
    full = full.reshape(groups, time_dev * keep, groups, rank * keep)
    own = np.stack([full[g, :, g] for g in range(groups)])
    high, low = split(full.reshape(groups, time_dev * keep, -1))
    image = np.concatenate([high, low, split(own)[0]], axis=-1)
    inner = np.stack([right[:rank] for _, right, _ in parts])
    inner = inner.reshape(groups, rank, 2, bins_dev).transpose(0, 2, 1, 3)
    return image, np.repeat(inner, keep, axis=2).reshape(groups, -1, bins_dev), rank


def body(
    cfg,
    series_hbm,
    kernel_hbm,
    prior_hbm,
    scale_hbm,
    short_hbm,
    tabs_hbm,
    img_hbm,
    out_ref,
    kbufs,
    rows,
    prior,
    scale,
    short,
    tabs,
    img_tab,
    inner,
    squeezed,
    arrived,
    spread,
    ebuf,
    left_mat,
    sbuf,
    rbuf,
    relay,
    joined,
    gath,
    lows,
    scaled,
    edges,
    halo_left,
    halo_right,
    small_sem,
    k_sem,
    g_send,
    g_recv,
    z_send,
    z_recv,
    relay_recv,
    x_send,
    x_recv,
    hl_send,
    hl_recv,
    hr_send,
    hr_recv,
    ready_x,
    ready_z,
    ready_far,
):
    groups, params, senses, chunks, direct, bins_dev, probes, squeeze = cfg
    f = lax.axis_index("freq")
    k = lax.axis_index("param")
    s = lax.axis_index("sens")
    sens_dev = rows.shape[1]
    depth = kernel_hbm.shape[1]
    padded = left_mat.shape[1] // 2
    keep = probes // senses
    each = gath.shape[2]
    cols = scale.shape[1]
    count = len(chunks)
    has_left = k > 0
    has_right = k < params - 1
    has_under = s > 0
    has_over = s < senses - 1
    outer = jnp.logical_or(s == 0, s == senses - 1)
    within = jnp.logical_not(outer)
    pair = s + 1 - 2 * lax.rem(s, 2)
    across = senses - 1 - s
    other = senses - 1 - pair

    def freq_peer(d):
        return lax.rem(f + d, groups)

    def tell(sem, **where):
        pl.semaphore_signal(sem, inc=1, device_id=where, device_id_type=MESH)

    small = [
        pltpu.make_async_copy(series_hbm, rows, small_sem.at[0]),
        pltpu.make_async_copy(short_hbm, short, small_sem.at[1]),
        pltpu.make_async_copy(tabs_hbm.at[f], tabs, small_sem.at[2]),
        pltpu.make_async_copy(prior_hbm, prior, small_sem.at[3]),
        pltpu.make_async_copy(scale_hbm, scale, small_sem.at[4]),
        pltpu.make_async_copy(img_hbm.at[f], img_tab, small_sem.at[5]),
    ]
    for copy in small:
        copy.start()

    barrier = pltpu.get_barrier_semaphore()
    for d in range(1, groups):
        tell(barrier, freq=freq_peer(d))

    @pl.when(has_under)
    def _():
        tell(barrier, sens=s - 1)

    @pl.when(has_over)
    def _():
        tell(barrier, sens=s + 1)

    @pl.when(has_left)
    def _():
        tell(barrier, param=k - 1)

    @pl.when(has_right)
    def _():
        tell(barrier, param=k + 1)

    row = lax.broadcasted_iota(jnp.int32, spread.shape, 0)
    lane = lax.broadcasted_iota(jnp.int32, spread.shape, 1)
    spread[...] = jnp.where(lane // bins_dev == row, 1.0, 0.0).astype(BF16)
    for buf in kbufs:
        pad = jnp.zeros((padded - depth, buf.shape[1]), BF16)
        buf[depth:padded] = pad
        buf[padded + depth :] = pad

    small[0].wait()
    small[1].wait()
    loads = [
        [
            pltpu.make_async_copy(
                kernel_hbm.at[part, :, pl.ds(at, width)],
                kbufs[c].at[pl.ds(part * padded, depth)],
                k_sem.at[c, part],
            )
            for part in range(2)
        ]
        for c, (at, width) in enumerate(chunks)
    ]
    for group in loads:
        for copy in group:
            copy.start()

    series = rows[...]

    def shortened(g):
        return jnp.dot(short[g, 0], series, preferred_element_type=F32) + jnp.dot(
            short[g, 1], series, preferred_element_type=F32
        )

    for d in range(1, groups):
        g = freq_peer(d)
        squeezed[g] = shortened(g).astype(BF16)

    beside = [has_under, has_over, has_left, has_right]
    pl.semaphore_wait(barrier, groups - 1 + sum(jnp.where(b, 1, 0) for b in beside))

    def series_copy(target, slot):
        return pltpu.make_async_remote_copy(
            src_ref=squeezed.at[target],
            dst_ref=arrived.at[slot],
            send_sem=g_send,
            recv_sem=g_recv,
            device_id={"freq": target},
            device_id_type=MESH,
        )

    for d in range(1, groups):
        series_copy(freq_peer(d), f).start()
    for d in range(1, groups):
        tell(ready_x, freq=freq_peer(d))

    @pl.when(within)
    def _():
        tell(ready_z, sens=s - 1)
        tell(ready_z, sens=s + 1)

    for copy in small[2:]:
        copy.wait()
    norm = 1.0 / math.sqrt(bins_dev * groups)
    lane = lax.broadcasted_iota(jnp.int32, (8, STEP), 1) % bins_dev
    value = jnp.zeros((8, STEP), F32)
    for b in range(bins_dev):
        value = jnp.where(lane == b, prior[b] * norm, value)
    base = groups * 2 * squeeze
    for q in range(2):
        inner[q] = tabs[base + q * each : base + (q + 1) * each] * value[:1]

    cuts = [(at, min(STEP, padded - at)) for at in range(0, padded, STEP)]

    def expand(coefs, at, width):
        first = at // bins_dev // LANES * LANES
        last = min(first + LANES, sens_dev)
        return jnp.dot(
            coefs[:, first:last], spread[first:last, at : at + width], preferred_element_type=F32
        )

    def weighed(full, d, q, width):
        total = None
        for j in range(squeeze):
            at = (d * 2 + q) * squeeze + j
            term = full[j * probes : (j + 1) * probes] * tabs[at : at + 1, :width]
            total = term if total is None else total + term
        return total

    mine = shortened(f)
    high = mine.astype(BF16)
    low = (mine - high.astype(F32)).astype(BF16)
    mine = jnp.concatenate([high, low], axis=0)
    for at, width in cuts:
        full = expand(mine, at, width)
        full = full[: squeeze * probes] + full[squeeze * probes :]
        for q in range(2):
            ebuf[q, :, at : at + width] = weighed(full, 0, q, width)

    pl.semaphore_wait(ready_z, 1)

    @pl.when(within)
    def _():
        tell(ready_far, sens=pair)

    for copy in loads[0]:
        copy.wait()

    def series_done():
        return pltpu.make_async_remote_copy(
            src_ref=squeezed.at[pl.ds(0, groups - 1)],
            dst_ref=arrived.at[pl.ds(0, groups - 1)],
            send_sem=g_send,
            recv_sem=g_recv,
            device_id={"freq": freq_peer(1)},
            device_id_type=MESH,
        )

    series_done().wait_recv()
    came = [arrived[freq_peer(d)] for d in range(1, groups)]
    for at, width in cuts:
        cut = slice(at, at + width)
        fulls = [expand(c, at, width) for c in came]
        for q in range(2):
            total = ebuf[q, :, cut]
            for d in range(1, groups):
                total = total + weighed(fulls[d - 1], d, q, width)
            ebuf[q, :, cut] = total
        which = lax.broadcasted_iota(jnp.int32, (8, width), 0) % keep
        for j in range(senses):
            both = []
            for q in range(2):
                e = jnp.broadcast_to(ebuf[q, j * keep : j * keep + 1, cut], (8, width))
                for r in range(1, keep):
                    here = j * keep + r
                    e = jnp.where(which == r, ebuf[q, here : here + 1, cut], e)
                both.append(jnp.concatenate([e] * (each // 8), axis=0))
            re, im = both
            one, two = inner[0, :, :width], inner[1, :, :width]
            block = slice(j * each, (j + 1) * each)
            left_mat[block, cut] = (one * re + two * im).astype(BF16)
            left_mat[block, padded + at : padded + at + width] = (one * im - two * re).astype(BF16)

    def blocks(c):
        at, width = chunks[c]
        return pl.ds(at // LANES, width // LANES)

    def remote(src, dst, send, recv, **where):
        return pltpu.make_async_remote_copy(
            src_ref=src,
            dst_ref=dst,
            send_sem=send,
            recv_sem=recv,
            device_id=where,
            device_id_type=MESH,
        )

    def z_copy(target, c):
        return remote(
            sbuf.at[target, blocks(c)], rbuf.at[s, blocks(c)], z_send, z_recv.at[c], sens=target
        )

    def z_done(units, c):
        part = rbuf.at[pl.ds(0, units), blocks(c)]
        return remote(part, part, z_send, z_recv.at[c], sens=pair)

    def relay_copy(c):
        return remote(
            sbuf.at[other, blocks(c)], relay.at[blocks(c)], z_send, relay_recv.at[c], sens=pair
        )

    def joined_copy(c):
        return remote(
            joined.at[blocks(c)], rbuf.at[s, blocks(c)], z_send, z_recv.at[c], sens=across
        )

    def send_sums(c):
        if c in direct:
            for target in (across, other, pair):
                z_copy(target, c).start()
            return

        @pl.when(outer)
        def _():
            relay_copy(c).start()
            z_copy(across, c).start()
            z_copy(pair, c).start()

        @pl.when(within)
        def _():
            z_copy(other, c).start()
            z_copy(pair, c).start()

    def pass_on(c):
        if c in direct:
            return

        @pl.when(within)
        def _():
            relay_copy(c).wait_recv()
            both = sbuf[across, blocks(c)].astype(F32) + relay[blocks(c)].astype(F32)
            joined[blocks(c)] = both.astype(BF16)
            joined_copy(c).start()

    def collect(c):
        if c in direct:
            z_done(3, c).wait_recv()
        else:

            @pl.when(outer)
            def _():
                z_done(3, c).wait_recv()

            @pl.when(within)
            def _():
                z_done(2, c).wait_recv()

        total = sbuf[s, blocks(c)].astype(F32)
        for slot in (pair, other, across):
            total = total + rbuf[slot, blocks(c)].astype(F32)
        return total

    @pl.when(within)
    def _():
        rbuf[other] = jnp.zeros(rbuf.shape[1:], BF16)

    for c, (at, width) in enumerate(chunks):
        if c > 0:
            for copy in loads[c]:
                copy.wait()
        total = jnp.dot(left_mat[...], kbufs[c][...], preferred_element_type=F32)
        total = total.astype(BF16)
        for j in range(senses):
            for b in range(width // LANES):
                sbuf[j, at // LANES + b] = total[
                    j * each : (j + 1) * each, b * LANES : (b + 1) * LANES
                ]
        if c == 0:

            @pl.when(outer)
            def _():
                pl.semaphore_wait(ready_far, 1)

        send_sums(c)

    def x_copy(target, c):
        part = gath.at[f, blocks(c)]
        return remote(part, part, x_send, x_recv.at[c], freq=target)

    def x_done(c):
        part = gath.at[pl.ds(0, groups - 1), blocks(c)]
        return remote(part, part, x_send, x_recv.at[c], freq=freq_peer(1))

    def to_left(target):
        return remote(
            edges.at[0],
            halo_right.at[f],
            hl_send,
            hr_recv,
            freq=target,
            param=jnp.maximum(k - 1, 0),
        )

    def to_right(target):
        return remote(
            edges.at[1],
            halo_left.at[f],
            hr_send,
            hl_recv,
            freq=target,
            param=jnp.minimum(k + 1, params - 1),
        )

    def image_of(stack, low):
        wide = 2 * groups * each
        full = jnp.concatenate(stack + stack + ([] if low is None else [low]), axis=0)
        table = img_tab[:, : wide if low is None else wide + each]
        return jnp.dot(table, full, preferred_element_type=F32)

    def across_lanes(parts):
        return parts[0] if len(parts) == 1 else jnp.concatenate(parts, axis=1)

    def finish(c):
        x_done(c).wait_recv()
        at, width = chunks[c]
        span = range(at // LANES, (at + width) // LANES)
        stack = [across_lanes([gath[g, b] for b in span]) for g in range(groups)]
        image = image_of(stack, across_lanes([lows[b] for b in span]))
        scaled[:, at : at + width] = image * scale[:, at : at + width]

    pl.semaphore_wait(ready_x, groups - 1)
    pass_on(0)
    for c, (at, width) in enumerate(chunks):
        if c + 1 < count:
            pass_on(c + 1)
        total = collect(c)
        high = total.astype(BF16)
        gath[f, blocks(c)] = high
        for d in range(1, groups):
            x_copy(freq_peer(d), c).start()
        lows[blocks(c)] = (total - high.astype(F32)).astype(BF16)
        if at == 0:
            edges[0] = (total[0] * scale[:, :LANES]).astype(BF16)

            @pl.when(has_left)
            def _():
                for d in range(groups):
                    to_left(freq_peer(d)).start()

        if at + width == cols:
            edges[1] = (total[width // LANES - 1] * scale[:, cols - LANES :]).astype(BF16)

            @pl.when(has_right)
            def _():
                for d in range(groups):
                    to_right(freq_peer(d)).start()

        if c >= 2:
            finish(c - 2)

    def halo_done(ref, send, recv):
        return remote(ref, ref, send, recv, freq=freq_peer(1))

    @pl.when(has_left)
    def _():
        halo_done(halo_left, hr_send, hl_recv).wait_recv()

    @pl.when(jnp.logical_not(has_left))
    def _():
        halo_left[...] = jnp.zeros_like(halo_left)

    @pl.when(has_right)
    def _():
        halo_done(halo_right, hl_send, hr_recv).wait_recv()

    @pl.when(jnp.logical_not(has_right))
    def _():
        halo_right[...] = jnp.zeros_like(halo_right)

    left = image_of([halo_left[g] for g in range(groups)], None)
    right = image_of([halo_right[g] for g in range(groups)], None)
    for c in range(max(count - 2, 0), count):
        finish(c)

    for at in range(0, cols, STEP):
        end = at + STEP
        mid = scaled[:, at:end]
        before = scaled[:, at - 1 : at] if at > 0 else left[:, LANES - 1 :]
        after = scaled[:, end : end + 1] if end < cols else right[:, :1]
        lower = jnp.concatenate([before, mid[:, :-1]], axis=1)
        upper = jnp.concatenate([mid[:, 1:], after], axis=1)
        value = scale[:, at:end] * (0.5 * mid + 0.25 * (lower + upper))
        out_ref[:, :, at:end] = value.reshape(out_ref.shape[0], keep, STEP)

    series_done().wait_send()
    part = sbuf.at[pl.ds(0, 3)]
    remote(part, part, z_send, z_recv.at[0], sens=pair).wait_send()
    part = gath.at[pl.ds(0, groups - 1)]
    remote(part, part, x_send, x_recv.at[0], freq=freq_peer(1)).wait_send()

    @pl.when(has_left)
    def _():
        halo_done(halo_right, hl_send, hr_recv).wait_send()

    @pl.when(has_right)
    def _():
        halo_done(halo_left, hr_send, hl_recv).wait_send()


def local(mesh_shape, series, kernel, prior_spectrum, prior_scale):
    groups, params, senses = (mesh_shape[n] for n in ("freq", "param", "sens"))
    assert senses == 4 and groups > 1
    probes, sens_dev, time_dev = series.shape
    _, bins_dev, _, cols = kernel.shape
    keep = probes // senses
    quarter = cols // 4
    chunks = [(0, quarter), (3 * quarter, quarter), (quarter, quarter), (2 * quarter, quarter)]
    direct = ()
    count = len(chunks)
    depth = sens_dev * bins_dev
    padded = -(-depth // LANES) * LANES
    short, long, squeeze = series_tables(groups, bins_dev, time_dev, probes)
    img_tab, inner, rank = image_tables(groups, bins_dev, time_dev, keep)
    tabs = np.concatenate([long, inner], axis=1)
    tabs = np.tile(tabs, (1, 1, STEP // bins_dev)).astype(np.float32)
    each = rank * keep
    spans = cols // LANES
    dma = pltpu.SemaphoreType.DMA
    plain = pltpu.SemaphoreType.REGULAR
    return pl.pallas_call(
        functools.partial(
            body, (groups, params, senses, chunks, direct, bins_dev, probes, squeeze)
        ),
        out_shape=pltpu.VMEM((time_dev, keep, cols), F32),
        in_specs=[pl.BlockSpec(memory_space=pltpu.HBM)] * 7,
        out_specs=pl.BlockSpec(memory_space=pltpu.VMEM),
        scratch_shapes=[
            [pltpu.VMEM((2 * padded, width), BF16) for _, width in chunks],
            pltpu.VMEM((time_dev * probes, sens_dev), BF16),
            pltpu.SMEM((bins_dev,), F32),
            pltpu.VMEM((1, cols), F32),
            pltpu.VMEM(short.shape, BF16),
            pltpu.VMEM(tabs.shape[1:], F32),
            pltpu.VMEM(img_tab.shape[1:], BF16),
            pltpu.VMEM((2, each, STEP), F32),
            pltpu.VMEM((groups, squeeze * probes, sens_dev), BF16),
            pltpu.VMEM((groups, squeeze * probes, sens_dev), BF16),
            pltpu.VMEM((sens_dev, padded), BF16),
            pltpu.VMEM((2, probes, padded), F32),
            pltpu.VMEM((senses * each, 2 * padded), BF16),
            pltpu.VMEM((senses, spans, each, LANES), BF16),
            pltpu.VMEM((senses, spans, each, LANES), BF16),
            pltpu.VMEM((spans, each, LANES), BF16),
            pltpu.VMEM((spans, each, LANES), BF16),
            pltpu.VMEM((groups, spans, each, LANES), BF16),
            pltpu.VMEM((spans, each, LANES), BF16),
            pltpu.VMEM((time_dev * keep, cols), F32),
            pltpu.VMEM((2, each, LANES), BF16),
            pltpu.VMEM((groups, each, LANES), BF16),
            pltpu.VMEM((groups, each, LANES), BF16),
            dma((6,)),
            dma((count, 2)),
            dma,
            dma,
            dma,
            dma((count,)),
            dma((count,)),
            dma,
            dma((count,)),
            dma,
            dma,
            dma,
            dma,
            plain,
            plain,
            plain,
        ],
        compiler_params=pltpu.CompilerParams(
            collective_id=0, has_side_effects=True, vmem_limit_bytes=60 * 1024 * 1024
        ),
    )(
        series.transpose(2, 0, 1).reshape(time_dev * probes, sens_dev),
        kernel.transpose(0, 2, 1, 3).reshape(2, depth, cols),
        prior_spectrum,
        prior_scale.reshape(1, cols),
        jnp.asarray(short),
        jnp.asarray(tabs),
        jnp.asarray(img_tab),
    )


def solution(mesh):
    placed = (P(None, "sens", "freq"), P(None, "freq", "sens", "param"), P("freq"), P("param"))
    return jax.shard_map(
        functools.partial(local, dict(mesh.shape)),
        mesh=mesh,
        in_specs=placed,
        out_specs=P("freq", "sens", "param"),
        check_vma=False,
    )
```

time: 23.7 us -> 20.6 us (0.87)
  the two profiles are of different devices: /device:TPU:8 before, /device:TPU:0 now
where the time goes in v2:
time: 20.6 us; the launch traced here: 20.5 us
  Pallas kernels  19.8 us (96%)
  local copies, waits for them, and re-layouts  0.69 us (3%)
    pallas_call x1, Pallas kernels, local(): pl.pallas_call(functools.partial(body, (groups, params, senses, chunks, d...  19.8 us
    unnamed x1, local copies, waits for them, and re-layouts  0.69 us

profile of v2, /device:TPU:0, one launch (start us, length us, event | category | flops | bytes accessed | tf_op | source)
XLA Modules:
  0.0 20.5 jit_solution(14802465329965815307)
XLA Ops:
  0.0 19.8 %shard_map.73 = f32[26,2,1024]{2,1,0:T(2,128)S(1)} custom-call(bf16[208,150]{1,0:T(8,128)(2,1)} %bitcast.8, bf16[2,2400,1024]{2,1,0:T(8,128)(2,1)} %bitcast.7, f32[16]{0:T(128)} %prior_hbm.1, f32[1,1024]{1,0:T(1,128)} %bitcast.9, bf16[2,2,80,208]{3,2,1,0:T(8,128)(2,1)} %constant.6.clone.short_hbm, f32[2,104,256]{2,1,0:T(8,128)} %constant.7.clone.tabs_hbm, ...), custom_call_target="tpu_custom_call" | custom-call | tf_op jit(solution)/shard_map/pallas_call | solution.py:577
  19.8 0.7 %copy.9 = f32[26,2,1024]{2,1,0:T(2,128)} copy(f32[26,2,1024]{2,1,0:T(2,128)S(1)} %shard_map.73) | data formatting | bytes 425984

commit v3 on v2

--- a/solution.py
+++ b/solution.py
@@ -146,6 +146,8 @@
     has_over = s < senses - 1
     outer = jnp.logical_or(s == 0, s == senses - 1)
     within = jnp.logical_not(outer)
+    second = lax.rem(k, 2) == 1
+    first = jnp.logical_not(second)
     pair = s + 1 - 2 * lax.rem(s, 2)
     across = senses - 1 - s
     other = senses - 1 - pair
@@ -303,30 +305,47 @@
             device_id_type=MESH,
         )
 
+    @pl.when(within)
+    def _():
+        for c, (at, width) in enumerate(chunks):
+            if c not in direct:
+                nothing = jnp.zeros((width // LANES,) + rbuf.shape[2:], BF16)
+                rbuf[other, pl.ds(at // LANES, width // LANES)] = nothing
+
     series_done().wait_recv()
     came = [arrived[freq_peer(d)] for d in range(1, groups)]
-    for at, width in cuts:
-        cut = slice(at, at + width)
-        fulls = [expand(c, at, width) for c in came]
-        for q in range(2):
-            total = ebuf[q, :, cut]
-            for d in range(1, groups):
-                total = total + weighed(fulls[d - 1], d, q, width)
-            ebuf[q, :, cut] = total
-        which = lax.broadcasted_iota(jnp.int32, (8, width), 0) % keep
-        for j in range(senses):
-            both = []
+    head = None
+    for group in [cuts[i : i + 2] for i in range(0, len(cuts), 2)]:
+        for at, width in group:
+            cut = slice(at, at + width)
+            fulls = [expand(c, at, width) for c in came]
             for q in range(2):
-                e = jnp.broadcast_to(ebuf[q, j * keep : j * keep + 1, cut], (8, width))
-                for r in range(1, keep):
-                    here = j * keep + r
-                    e = jnp.where(which == r, ebuf[q, here : here + 1, cut], e)
-                both.append(jnp.concatenate([e] * (each // 8), axis=0))
-            re, im = both
-            one, two = inner[0, :, :width], inner[1, :, :width]
-            block = slice(j * each, (j + 1) * each)
-            left_mat[block, cut] = (one * re + two * im).astype(BF16)
-            left_mat[block, padded + at : padded + at + width] = (one * im - two * re).astype(BF16)
+                total = ebuf[q, :, cut]
+                for d in range(1, groups):
+                    total = total + weighed(fulls[d - 1], d, q, width)
+                ebuf[q, :, cut] = total
+            which = lax.broadcasted_iota(jnp.int32, (8, width), 0) % keep
+            for j in range(senses):
+                both = []
+                for q in range(2):
+                    e = jnp.broadcast_to(ebuf[q, j * keep : j * keep + 1, cut], (8, width))
+                    for r in range(1, keep):
+                        here = j * keep + r
+                        e = jnp.where(which == r, ebuf[q, here : here + 1, cut], e)
+                    both.append(jnp.concatenate([e] * (each // 8), axis=0))
+                re, im = both
+                one, two = inner[0, :, :width], inner[1, :, :width]
+                block = slice(j * each, (j + 1) * each)
+                left_mat[block, cut] = (one * re + two * im).astype(BF16)
+                left_mat[block, padded + at : padded + at + width] = (one * im - two * re).astype(BF16)
+        start, stop = group[0][0], group[-1][0] + group[-1][1]
+        for base in (0, padded):
+            term = jnp.dot(
+                left_mat[:, base + start : base + stop],
+                kbufs[0][base + start : base + stop],
+                preferred_element_type=F32,
+            )
+            head = term if head is None else head + term
 
     def blocks(c):
         at, width = chunks[c]
@@ -407,15 +426,13 @@
             total = total + rbuf[slot, blocks(c)].astype(F32)
         return total
 
-    @pl.when(within)
-    def _():
-        rbuf[other] = jnp.zeros(rbuf.shape[1:], BF16)
-
     for c, (at, width) in enumerate(chunks):
         if c > 0:
             for copy in loads[c]:
                 copy.wait()
-        total = jnp.dot(left_mat[...], kbufs[c][...], preferred_element_type=F32)
+        total = head
+        if c > 0:
+            total = jnp.dot(left_mat[...], kbufs[c][...], preferred_element_type=F32)
         total = total.astype(BF16)
         for j in range(senses):
             for b in range(width // LANES):
@@ -476,10 +493,9 @@
         scaled[:, at : at + width] = image * scale[:, at : at + width]
 
     pl.semaphore_wait(ready_x, groups - 1)
-    pass_on(0)
+    for c in range(count):
+        pass_on(c)
     for c, (at, width) in enumerate(chunks):
-        if c + 1 < count:
-            pass_on(c + 1)
         total = collect(c)
         high = total.astype(BF16)
         gath[f, blocks(c)] = high
@@ -502,8 +518,8 @@
                 for d in range(groups):
                     to_right(freq_peer(d)).start()
 
-        if c >= 2:
-            finish(c - 2)
+    for c in range(count - 1):
+        finish(c)
 
     def halo_done(ref, send, recv):
         return remote(ref, ref, send, recv, freq=freq_peer(1))
@@ -526,18 +542,23 @@
 
     left = image_of([halo_left[g] for g in range(groups)], None)
     right = image_of([halo_right[g] for g in range(groups)], None)
-    for c in range(max(count - 2, 0), count):
-        finish(c)
-
-    for at in range(0, cols, STEP):
-        end = at + STEP
+    def smooth(at, end):
+        if at >= end:
+            return
         mid = scaled[:, at:end]
         before = scaled[:, at - 1 : at] if at > 0 else left[:, LANES - 1 :]
         after = scaled[:, end : end + 1] if end < cols else right[:, :1]
         lower = jnp.concatenate([before, mid[:, :-1]], axis=1)
         upper = jnp.concatenate([mid[:, 1:], after], axis=1)
         value = scale[:, at:end] * (0.5 * mid + 0.25 * (lower + upper))
-        out_ref[:, :, at:end] = value.reshape(out_ref.shape[0], keep, STEP)
+        out_ref[:, :, at:end] = value.reshape(out_ref.shape[0], keep, end - at)
+
+    at, width = chunks[-1]
+    start, stop = max(at - LANES, 0), min(at + width + LANES, cols)
+    smooth(0, start)
+    smooth(stop, cols)
+    finish(count - 1)
+    smooth(start, stop)
 
     series_done().wait_send()
     part = sbuf.at[pl.ds(0, 3)]
@@ -562,7 +583,7 @@
     keep = probes // senses
     quarter = cols // 4
     chunks = [(0, quarter), (3 * quarter, quarter), (quarter, quarter), (2 * quarter, quarter)]
-    direct = ()
+    direct = (len(chunks) - 1,)
     count = len(chunks)
     depth = sens_dev * bins_dev
     padded = -(-depth // LANES) * LANES

time: 20.6 us -> 19.1 us (0.927)
  Pallas kernels: 19.8 us -> 18.3 us
    pallas_call x1, Pallas kernels: 19.8 us -> 18.3 us  [local(): pl.pallas_call(functools.partial(body, (groups, params, senses, chunks, d...]
where the time goes in v3:
time: 19.1 us; the launch traced here: 19 us
  Pallas kernels  18.3 us (96%)
  local copies, waits for them, and re-layouts  0.69 us (4%)
    pallas_call x1, Pallas kernels, local(): pl.pallas_call(functools.partial(body, (groups, params, senses, chunks, d...  18.3 us
    unnamed x1, local copies, waits for them, and re-layouts  0.69 us

profile of v3, /device:TPU:0, one launch (start us, length us, event | category | flops | bytes accessed | tf_op | source)
XLA Modules:
  0.0 19.0 jit_solution(16730275114279607647)
XLA Ops:
  0.0 18.3 %shard_map.73 = f32[26,2,1024]{2,1,0:T(2,128)S(1)} custom-call(bf16[208,150]{1,0:T(8,128)(2,1)} %bitcast.8, bf16[2,2400,1024]{2,1,0:T(8,128)(2,1)} %bitcast.7, f32[16]{0:T(128)} %prior_hbm.1, f32[1,1024]{1,0:T(1,128)} %bitcast.9, bf16[2,2,80,208]{3,2,1,0:T(8,128)(2,1)} %constant.6.clone.short_hbm, f32[2,104,256]{2,1,0:T(8,128)} %constant.7.clone.tabs_hbm, ...), custom_call_target="tpu_custom_call" | custom-call | tf_op jit(solution)/shard_map/pallas_call | solution.py:598
  18.3 0.7 %copy.9 = f32[26,2,1024]{2,1,0:T(2,128)} copy(f32[26,2,1024]{2,1,0:T(2,128)S(1)} %shard_map.73) | data formatting | bytes 425984

commit v4 on v3

--- a/solution.py
+++ b/solution.py
@@ -63,20 +63,35 @@
     return short, long.reshape(groups, -1, bins_dev), rank
 
 
+def packing(each):
+    whole = each // 8 * 8
+    first = np.concatenate([np.arange(whole), 2 * whole + np.arange(each - whole)])
+    second = np.concatenate([whole + np.arange(whole), whole + each + np.arange(each - whole)])
+    return first, second
+
+
 def image_tables(groups, bins_dev, time_dev, keep):
     comps = phases(groups, bins_dev, time_dev)
-    parts = [factor(comp, 8) for comp in comps]
+    parts = [factor(comp, 2) for comp in comps]
     rank = max(part[2] for part in parts)
+    each, rows = rank * keep, time_dev * keep
     outer = np.stack([left[:, :rank] for left, _, _ in parts])
-    outer = outer.reshape(groups, groups, time_dev, rank).transpose(1, 2, 0, 3)
-    full = np.einsum("gthj,qr->gtqhjr", outer, np.eye(keep))
-    full = full.reshape(groups, time_dev * keep, groups, rank * keep)
-    own = np.stack([full[g, :, g] for g in range(groups)])
-    high, low = split(full.reshape(groups, time_dev * keep, -1))
-    image = np.concatenate([high, low, split(own)[0]], axis=-1)
+    outer = outer.reshape(groups, groups, time_dev, rank).transpose(1, 0, 2, 3)
+    full = np.einsum("ghtj,qr->ghtqjr", outer, np.eye(keep))
+    full = full.reshape(groups, groups, rows, each)
+    tall = -(-rows // 8) * 8
+    packed = np.zeros((groups, groups, 2 * tall, 2 * each))
+    for half, places in enumerate(packing(each)):
+        packed[:, :, half * tall : half * tall + rows, places] = full
+    high, low = split(packed)
+    own = np.stack([high[g, g] for g in range(groups)])
+    image = np.concatenate([high, low, own[:, None]], axis=1)
     inner = np.stack([right[:rank] for _, right, _ in parts])
     inner = inner.reshape(groups, rank, 2, bins_dev).transpose(0, 2, 1, 3)
-    return image, np.repeat(inner, keep, axis=2).reshape(groups, -1, bins_dev), rank
+    inner = np.repeat(inner, keep, axis=2)
+    slot = -(-each // 8) * 8
+    inner = np.pad(inner, ((0, 0), (0, 0), (0, slot - each), (0, 0)))
+    return image, inner.reshape(groups, -1, bins_dev), each, slot
 
 
 def body(
@@ -129,7 +144,7 @@
     ready_z,
     ready_far,
 ):
-    groups, params, senses, chunks, direct, bins_dev, probes, squeeze = cfg
+    groups, params, senses, chunks, direct, bins_dev, probes, squeeze, each = cfg
     f = lax.axis_index("freq")
     k = lax.axis_index("param")
     s = lax.axis_index("sens")
@@ -137,7 +152,8 @@
     depth = kernel_hbm.shape[1]
     padded = left_mat.shape[1] // 2
     keep = probes // senses
-    each = gath.shape[2]
+    slot = inner.shape[1]
+    width = 2 * LANES
     cols = scale.shape[1]
     count = len(chunks)
     has_left = k > 0
@@ -208,7 +224,7 @@
             )
             for part in range(2)
         ]
-        for c, (at, width) in enumerate(chunks)
+        for c, at in enumerate(chunks)
     ]
     for group in loads:
         for copy in group:
@@ -257,22 +273,22 @@
         value = jnp.where(lane == b, prior[b] * norm, value)
     base = groups * 2 * squeeze
     for q in range(2):
-        inner[q] = tabs[base + q * each : base + (q + 1) * each] * value[:1]
+        inner[q] = tabs[base + q * slot : base + (q + 1) * slot] * value[:1]
 
     cuts = [(at, min(STEP, padded - at)) for at in range(0, padded, STEP)]
 
-    def expand(coefs, at, width):
+    def expand(coefs, at, span):
         first = at // bins_dev // LANES * LANES
         last = min(first + LANES, sens_dev)
         return jnp.dot(
-            coefs[:, first:last], spread[first:last, at : at + width], preferred_element_type=F32
-        )
-
-    def weighed(full, d, q, width):
+            coefs[:, first:last], spread[first:last, at : at + span], preferred_element_type=F32
+        )
+
+    def weighed(full, d, q, span):
         total = None
         for j in range(squeeze):
             at = (d * 2 + q) * squeeze + j
-            term = full[j * probes : (j + 1) * probes] * tabs[at : at + 1, :width]
+            term = full[j * probes : (j + 1) * probes] * tabs[at : at + 1, :span]
             total = term if total is None else total + term
         return total
 
@@ -280,11 +296,11 @@
     high = mine.astype(BF16)
     low = (mine - high.astype(F32)).astype(BF16)
     mine = jnp.concatenate([high, low], axis=0)
-    for at, width in cuts:
-        full = expand(mine, at, width)
+    for at, span in cuts:
+        full = expand(mine, at, span)
         full = full[: squeeze * probes] + full[squeeze * probes :]
         for q in range(2):
-            ebuf[q, :, at : at + width] = weighed(full, 0, q, width)
+            ebuf[q, :, at : at + span] = weighed(full, 0, q, span)
 
     pl.semaphore_wait(ready_z, 1)
 
@@ -307,37 +323,36 @@
 
     @pl.when(within)
     def _():
-        for c, (at, width) in enumerate(chunks):
+        for c in range(count):
             if c not in direct:
-                nothing = jnp.zeros((width // LANES,) + rbuf.shape[2:], BF16)
-                rbuf[other, pl.ds(at // LANES, width // LANES)] = nothing
+                rbuf[other, c] = jnp.zeros(rbuf.shape[2:], BF16)
 
     series_done().wait_recv()
     came = [arrived[freq_peer(d)] for d in range(1, groups)]
     head = None
     for group in [cuts[i : i + 2] for i in range(0, len(cuts), 2)]:
-        for at, width in group:
-            cut = slice(at, at + width)
-            fulls = [expand(c, at, width) for c in came]
+        for at, span in group:
+            cut = slice(at, at + span)
+            fulls = [expand(c, at, span) for c in came]
             for q in range(2):
                 total = ebuf[q, :, cut]
                 for d in range(1, groups):
-                    total = total + weighed(fulls[d - 1], d, q, width)
+                    total = total + weighed(fulls[d - 1], d, q, span)
                 ebuf[q, :, cut] = total
-            which = lax.broadcasted_iota(jnp.int32, (8, width), 0) % keep
+            which = lax.broadcasted_iota(jnp.int32, (8, span), 0) % keep
             for j in range(senses):
                 both = []
                 for q in range(2):
-                    e = jnp.broadcast_to(ebuf[q, j * keep : j * keep + 1, cut], (8, width))
+                    e = jnp.broadcast_to(ebuf[q, j * keep : j * keep + 1, cut], (8, span))
                     for r in range(1, keep):
                         here = j * keep + r
                         e = jnp.where(which == r, ebuf[q, here : here + 1, cut], e)
-                    both.append(jnp.concatenate([e] * (each // 8), axis=0))
+                    both.append(jnp.concatenate([e] * (slot // 8), axis=0))
                 re, im = both
-                one, two = inner[0, :, :width], inner[1, :, :width]
-                block = slice(j * each, (j + 1) * each)
+                one, two = inner[0, :, :span], inner[1, :, :span]
+                block = slice(j * slot, (j + 1) * slot)
                 left_mat[block, cut] = (one * re + two * im).astype(BF16)
-                left_mat[block, padded + at : padded + at + width] = (one * im - two * re).astype(BF16)
+                left_mat[block, padded + at : padded + at + span] = (one * im - two * re).astype(BF16)
         start, stop = group[0][0], group[-1][0] + group[-1][1]
         for base in (0, padded):
             term = jnp.dot(
@@ -347,10 +362,6 @@
             )
             head = term if head is None else head + term
 
-    def blocks(c):
-        at, width = chunks[c]
-        return pl.ds(at // LANES, width // LANES)
-
     def remote(src, dst, send, recv, **where):
         return pltpu.make_async_remote_copy(
             src_ref=src,
@@ -363,21 +374,21 @@
 
     def z_copy(target, c):
         return remote(
-            sbuf.at[target, blocks(c)], rbuf.at[s, blocks(c)], z_send, z_recv.at[c], sens=target
+            sbuf.at[target, c], rbuf.at[s, c], z_send, z_recv.at[c], sens=target
         )
 
     def z_done(units, c):
-        part = rbuf.at[pl.ds(0, units), blocks(c)]
+        part = rbuf.at[pl.ds(0, units), c]
         return remote(part, part, z_send, z_recv.at[c], sens=pair)
 
     def relay_copy(c):
         return remote(
-            sbuf.at[other, blocks(c)], relay.at[blocks(c)], z_send, relay_recv.at[c], sens=pair
+            sbuf.at[other, c], relay.at[c], z_send, relay_recv.at[c], sens=pair
         )
 
     def joined_copy(c):
         return remote(
-            joined.at[blocks(c)], rbuf.at[s, blocks(c)], z_send, z_recv.at[c], sens=across
+            joined.at[c], rbuf.at[s, c], z_send, z_recv.at[c], sens=across
         )
 
     def send_sums(c):
@@ -404,8 +415,8 @@
         @pl.when(within)
         def _():
             relay_copy(c).wait_recv()
-            both = sbuf[across, blocks(c)].astype(F32) + relay[blocks(c)].astype(F32)
-            joined[blocks(c)] = both.astype(BF16)
+            both = sbuf[across, c].astype(F32) + relay[c].astype(F32)
+            joined[c] = both.astype(BF16)
             joined_copy(c).start()
 
     def collect(c):
@@ -421,24 +432,27 @@
             def _():
                 z_done(2, c).wait_recv()
 
-        total = sbuf[s, blocks(c)].astype(F32)
+        total = sbuf[s, c].astype(F32)
         for slot in (pair, other, across):
-            total = total + rbuf[slot, blocks(c)].astype(F32)
+            total = total + rbuf[slot, c].astype(F32)
         return total
 
-    for c, (at, width) in enumerate(chunks):
+    whole = each // 8 * 8
+    for c in range(count):
         if c > 0:
             for copy in loads[c]:
                 copy.wait()
         total = head
         if c > 0:
             total = jnp.dot(left_mat[...], kbufs[c][...], preferred_element_type=F32)
-        total = total.astype(BF16)
         for j in range(senses):
-            for b in range(width // LANES):
-                sbuf[j, at // LANES + b] = total[
-                    j * each : (j + 1) * each, b * LANES : (b + 1) * LANES
-                ]
+            halves = [
+                total[j * slot : (j + 1) * slot, h * LANES : (h + 1) * LANES] for h in range(2)
+            ]
+            packed = [half[:whole] for half in halves]
+            if slot > each:
+                packed.append(halves[0][whole:] + pltpu.roll(halves[1][whole:], each - whole, 0))
+            sbuf[j, c] = jnp.concatenate(packed, axis=0).astype(BF16)
         if c == 0:
 
             @pl.when(outer)
@@ -448,11 +462,11 @@
         send_sums(c)
 
     def x_copy(target, c):
-        part = gath.at[f, blocks(c)]
+        part = gath.at[f, c]
         return remote(part, part, x_send, x_recv.at[c], freq=target)
 
     def x_done(c):
-        part = gath.at[pl.ds(0, groups - 1), blocks(c)]
+        part = gath.at[pl.ds(0, groups - 1), c]
         return remote(part, part, x_send, x_recv.at[c], freq=freq_peer(1))
 
     def to_left(target):
@@ -475,35 +489,38 @@
             param=jnp.minimum(k + 1, params - 1),
         )
 
-    def image_of(stack, low):
-        wide = 2 * groups * each
-        full = jnp.concatenate(stack + stack + ([] if low is None else [low]), axis=0)
-        table = img_tab[:, : wide if low is None else wide + each]
-        return jnp.dot(table, full, preferred_element_type=F32)
-
-    def across_lanes(parts):
-        return parts[0] if len(parts) == 1 else jnp.concatenate(parts, axis=1)
+    rows_out = scaled.shape[0]
+    tall = img_tab.shape[1] // 2
+
+    def image_of(pieces):
+        total = None
+        for index, piece in pieces:
+            term = jnp.dot(img_tab[index], piece, preferred_element_type=F32)
+            total = term if total is None else total + term
+        return total[:rows_out], total[tall : tall + rows_out]
+
+    def twice(pieces):
+        return list(enumerate(pieces + pieces))
 
     def finish(c):
         x_done(c).wait_recv()
-        at, width = chunks[c]
-        span = range(at // LANES, (at + width) // LANES)
-        stack = [across_lanes([gath[g, b] for b in span]) for g in range(groups)]
-        image = image_of(stack, across_lanes([lows[b] for b in span]))
-        scaled[:, at : at + width] = image * scale[:, at : at + width]
+        pieces = twice([gath[g, c] for g in range(groups)]) + [(2 * groups, lows[c])]
+        for half, image in enumerate(image_of(pieces)):
+            at = chunks[c] + half * LANES
+            scaled[:, at : at + LANES] = image * scale[:, at : at + LANES]
 
     pl.semaphore_wait(ready_x, groups - 1)
     for c in range(count):
         pass_on(c)
-    for c, (at, width) in enumerate(chunks):
+    for c, at in enumerate(chunks):
         total = collect(c)
         high = total.astype(BF16)
-        gath[f, blocks(c)] = high
+        gath[f, c] = high
         for d in range(1, groups):
             x_copy(freq_peer(d), c).start()
-        lows[blocks(c)] = (total - high.astype(F32)).astype(BF16)
+        lows[c] = (total - high.astype(F32)).astype(BF16)
         if at == 0:
-            edges[0] = (total[0] * scale[:, :LANES]).astype(BF16)
+            edges[0] = (total * scale[:, :LANES]).astype(BF16)
 
             @pl.when(has_left)
             def _():
@@ -511,7 +528,7 @@
                     to_left(freq_peer(d)).start()
 
         if at + width == cols:
-            edges[1] = (total[width // LANES - 1] * scale[:, cols - LANES :]).astype(BF16)
+            edges[1] = (total * scale[:, cols - LANES :]).astype(BF16)
 
             @pl.when(has_right)
             def _():
@@ -540,8 +557,8 @@
     def _():
         halo_right[...] = jnp.zeros_like(halo_right)
 
-    left = image_of([halo_left[g] for g in range(groups)], None)
-    right = image_of([halo_right[g] for g in range(groups)], None)
+    _, left = image_of(twice([halo_left[g] for g in range(groups)]))
+    right, _ = image_of(twice([halo_right[g] for g in range(groups)]))
     def smooth(at, end):
         if at >= end:
             return
@@ -553,7 +570,7 @@
         value = scale[:, at:end] * (0.5 * mid + 0.25 * (lower + upper))
         out_ref[:, :, at:end] = value.reshape(out_ref.shape[0], keep, end - at)
 
-    at, width = chunks[-1]
+    at = chunks[-1]
     start, stop = max(at - LANES, 0), min(at + width + LANES, cols)
     smooth(0, start)
     smooth(stop, cols)
@@ -581,51 +598,52 @@
     probes, sens_dev, time_dev = series.shape
     _, bins_dev, _, cols = kernel.shape
     keep = probes // senses
-    quarter = cols // 4
-    chunks = [(0, quarter), (3 * quarter, quarter), (quarter, quarter), (2 * quarter, quarter)]
+    width = 2 * LANES
+    assert cols % width == 0
+    chunks = list(range(0, cols, width))
+    chunks = chunks[:1] + chunks[:0:-1][:1] + chunks[1:-1]
     direct = (len(chunks) - 1,)
     count = len(chunks)
     depth = sens_dev * bins_dev
     padded = -(-depth // LANES) * LANES
     short, long, squeeze = series_tables(groups, bins_dev, time_dev, probes)
-    img_tab, inner, rank = image_tables(groups, bins_dev, time_dev, keep)
+    img_tab, inner, each, slot = image_tables(groups, bins_dev, time_dev, keep)
     tabs = np.concatenate([long, inner], axis=1)
     tabs = np.tile(tabs, (1, 1, STEP // bins_dev)).astype(np.float32)
-    each = rank * keep
-    spans = cols // LANES
+    unit = (2 * each, LANES)
     dma = pltpu.SemaphoreType.DMA
     plain = pltpu.SemaphoreType.REGULAR
     return pl.pallas_call(
         functools.partial(
-            body, (groups, params, senses, chunks, direct, bins_dev, probes, squeeze)
+            body, (groups, params, senses, chunks, direct, bins_dev, probes, squeeze, each)
         ),
         out_shape=pltpu.VMEM((time_dev, keep, cols), F32),
         in_specs=[pl.BlockSpec(memory_space=pltpu.HBM)] * 7,
         out_specs=pl.BlockSpec(memory_space=pltpu.VMEM),
         scratch_shapes=[
-            [pltpu.VMEM((2 * padded, width), BF16) for _, width in chunks],
+            [pltpu.VMEM((2 * padded, width), BF16) for _ in chunks],
             pltpu.VMEM((time_dev * probes, sens_dev), BF16),
             pltpu.SMEM((bins_dev,), F32),
             pltpu.VMEM((1, cols), F32),
             pltpu.VMEM(short.shape, BF16),
             pltpu.VMEM(tabs.shape[1:], F32),
             pltpu.VMEM(img_tab.shape[1:], BF16),
-            pltpu.VMEM((2, each, STEP), F32),
+            pltpu.VMEM((2, slot, STEP), F32),
             pltpu.VMEM((groups, squeeze * probes, sens_dev), BF16),
             pltpu.VMEM((groups, squeeze * probes, sens_dev), BF16),
             pltpu.VMEM((sens_dev, padded), BF16),
             pltpu.VMEM((2, probes, padded), F32),
-            pltpu.VMEM((senses * each, 2 * padded), BF16),
-            pltpu.VMEM((senses, spans, each, LANES), BF16),
-            pltpu.VMEM((senses, spans, each, LANES), BF16),
-            pltpu.VMEM((spans, each, LANES), BF16),
-            pltpu.VMEM((spans, each, LANES), BF16),
-            pltpu.VMEM((groups, spans, each, LANES), BF16),
-            pltpu.VMEM((spans, each, LANES), BF16),
+            pltpu.VMEM((senses * slot, 2 * padded), BF16),
+            pltpu.VMEM((senses, count) + unit, BF16),
+            pltpu.VMEM((senses, count) + unit, BF16),
+            pltpu.VMEM((count,) + unit, BF16),
+            pltpu.VMEM((count,) + unit, BF16),
+            pltpu.VMEM((groups, count) + unit, BF16),
+            pltpu.VMEM((count,) + unit, BF16),
             pltpu.VMEM((time_dev * keep, cols), F32),
-            pltpu.VMEM((2, each, LANES), BF16),
-            pltpu.VMEM((groups, each, LANES), BF16),
-            pltpu.VMEM((groups, each, LANES), BF16),
+            pltpu.VMEM((2,) + unit, BF16),
+            pltpu.VMEM((groups,) + unit, BF16),
+            pltpu.VMEM((groups,) + unit, BF16),
             dma((6,)),
             dma((count, 2)),
             dma,

time: 19.1 us -> 19.2 us (level)
  no operation moved by 1% of the time
where the time goes in v4:
time: 19.2 us; the launch traced here: 19 us
  Pallas kernels  18.3 us (95%)
  local copies, waits for them, and re-layouts  0.69 us (4%)
    pallas_call x1, Pallas kernels, local(): pl.pallas_call(functools.partial(body, (groups, params, senses, chunks, d...  18.3 us
    unnamed x1, local copies, waits for them, and re-layouts  0.69 us

profile of v4, /device:TPU:0, one launch (start us, length us, event | category | flops | bytes accessed | tf_op | source)
XLA Modules:
  0.0 19.0 jit_solution(13321800291324224423)
XLA Ops:
  0.0 18.3 %shard_map.73 = f32[26,2,1024]{2,1,0:T(2,128)S(1)} custom-call(bf16[208,150]{1,0:T(8,128)(2,1)} %bitcast.8, bf16[2,2400,1024]{2,1,0:T(8,128)(2,1)} %bitcast.7, f32[16]{0:T(128)} %prior_hbm.1, f32[1,1024]{1,0:T(1,128)} %bitcast.9, bf16[2,2,80,208]{3,2,1,0:T(8,128)(2,1)} %constant.6.clone.short_hbm, f32[2,104,256]{2,1,0:T(8,128)} %constant.7.clone.tabs_hbm, ...), custom_call_target="tpu_custom_call" | custom-call | tf_op jit(solution)/shard_map/pallas_call | solution.py:616
  18.3 0.7 %copy.9 = f32[26,2,1024]{2,1,0:T(2,128)} copy(f32[26,2,1024]{2,1,0:T(2,128)S(1)} %shard_map.73) | data formatting | bytes 425984

commit v5 on v4

--- a/solution.py
+++ b/solution.py
@@ -16,6 +16,7 @@
 RESIDUAL = 2.0**-26
 STEP = 256
 LANES = 128
+PAIR = 16
 
 
 def split(table):
@@ -220,7 +221,7 @@
             pltpu.make_async_copy(
                 kernel_hbm.at[part, :, pl.ds(at, width)],
                 kbufs[c].at[pl.ds(part * padded, depth)],
-                k_sem.at[c, part],
+                k_sem.at[c],
             )
             for part in range(2)
         ]
@@ -237,9 +238,32 @@
             short[g, 1], series, preferred_element_type=F32
         )
 
+    main = sens_dev // LANES * LANES
+    rest = sens_dev - main
+    tall_rows = squeeze * probes
+    fit = LANES // rest
+
+    def fold(part):
+        lines = [part[i : i + PAIR] for i in range(0, tall_rows, PAIR)]
+        folded = []
+        for i in range(0, len(lines), fit):
+            some = lines[i : i + fit]
+            gap = jnp.zeros((PAIR, LANES - rest * len(some)), F32)
+            folded.append(jnp.concatenate(some + [gap], axis=1))
+        return folded
+
+    def unfold(packed):
+        parts = []
+        for i in range(tall_rows // PAIR):
+            line = packed[i // fit * PAIR : (i // fit + 1) * PAIR]
+            parts.append(line[:, i % fit * rest : (i % fit + 1) * rest])
+        return jnp.concatenate(parts, axis=0)
+
     for d in range(1, groups):
         g = freq_peer(d)
-        squeezed[g] = shortened(g).astype(BF16)
+        value = shortened(g)
+        wide = [value[:, i : i + LANES] for i in range(0, main, LANES)]
+        squeezed[g] = jnp.concatenate(wide + fold(value[:, main:]), axis=0).astype(BF16)
 
     beside = [has_under, has_over, has_left, has_right]
     pl.semaphore_wait(barrier, groups - 1 + sum(jnp.where(b, 1, 0) for b in beside))
@@ -277,12 +301,10 @@
 
     cuts = [(at, min(STEP, padded - at)) for at in range(0, padded, STEP)]
 
-    def expand(coefs, at, span):
-        first = at // bins_dev // LANES * LANES
-        last = min(first + LANES, sens_dev)
-        return jnp.dot(
-            coefs[:, first:last], spread[first:last, at : at + span], preferred_element_type=F32
-        )
+    def expand(parts, at, span):
+        first = at // bins_dev // LANES
+        rows_of = spread[first * LANES : min((first + 1) * LANES, sens_dev), at : at + span]
+        return jnp.dot(parts[first], rows_of, preferred_element_type=F32)
 
     def weighed(full, d, q, span):
         total = None
@@ -296,8 +318,9 @@
     high = mine.astype(BF16)
     low = (mine - high.astype(F32)).astype(BF16)
     mine = jnp.concatenate([high, low], axis=0)
+    mine_parts = [mine[:, i : min(i + LANES, sens_dev)] for i in range(0, sens_dev, LANES)]
     for at, span in cuts:
-        full = expand(mine, at, span)
+        full = expand(mine_parts, at, span)
         full = full[: squeeze * probes] + full[squeeze * probes :]
         for q in range(2):
             ebuf[q, :, at : at + span] = weighed(full, 0, q, span)
@@ -308,8 +331,11 @@
     def _():
         tell(ready_far, sens=pair)
 
-    for copy in loads[0]:
-        copy.wait()
+    def loaded(c):
+        part = kbufs[c].at[pl.ds(0, 2 * depth)]
+        pltpu.make_async_copy(part, part, k_sem.at[c]).wait()
+
+    loaded(0)
 
     def series_done():
         return pltpu.make_async_remote_copy(
@@ -328,7 +354,12 @@
                 rbuf[other, c] = jnp.zeros(rbuf.shape[2:], BF16)
 
     series_done().wait_recv()
-    came = [arrived[freq_peer(d)] for d in range(1, groups)]
+    came = []
+    for d in range(1, groups):
+        got = arrived.at[freq_peer(d)]
+        parts = [got[i * tall_rows : (i + 1) * tall_rows] for i in range(main // LANES)]
+        tail = got[main // LANES * tall_rows :].astype(F32)
+        came.append(parts + [unfold(tail).astype(BF16)])
     head = None
     for group in [cuts[i : i + 2] for i in range(0, len(cuts), 2)]:
         for at, span in group:
@@ -399,8 +430,8 @@
 
         @pl.when(outer)
         def _():
+            z_copy(across, c).start()
             relay_copy(c).start()
-            z_copy(across, c).start()
             z_copy(pair, c).start()
 
         @pl.when(within)
@@ -440,8 +471,7 @@
     whole = each // 8 * 8
     for c in range(count):
         if c > 0:
-            for copy in loads[c]:
-                copy.wait()
+            loaded(c)
         total = head
         if c > 0:
             total = jnp.dot(left_mat[...], kbufs[c][...], preferred_element_type=F32)
@@ -499,15 +529,24 @@
             total = term if total is None else total + term
         return total[:rows_out], total[tall : tall + rows_out]
 
-    def twice(pieces):
-        return list(enumerate(pieces + pieces))
+    def twice(g, piece):
+        return [(g, piece), (groups + g, piece)]
+
+    def begin(c):
+        pieces = twice(f, gath[f, c]) + [(2 * groups, lows[c])]
+        for half, image in enumerate(image_of(pieces)):
+            at = chunks[c] + half * LANES
+            scaled[:, at : at + LANES] = image
 
     def finish(c):
         x_done(c).wait_recv()
-        pieces = twice([gath[g, c] for g in range(groups)]) + [(2 * groups, lows[c])]
+        pieces = []
+        for d in range(1, groups):
+            pieces += twice(freq_peer(d), gath[freq_peer(d), c])
         for half, image in enumerate(image_of(pieces)):
             at = chunks[c] + half * LANES
-            scaled[:, at : at + LANES] = image * scale[:, at : at + LANES]
+            lanes = slice(at, at + LANES)
+            scaled[:, lanes] = (scaled[:, lanes] + image) * scale[:, lanes]
 
     pl.semaphore_wait(ready_x, groups - 1)
     for c in range(count):
@@ -535,30 +574,33 @@
                 for d in range(groups):
                     to_right(freq_peer(d)).start()
 
+    for c in range(count):
+        begin(c)
+
+    def halo_done(ref, send, recv):
+        return remote(ref, ref, send, recv, freq=freq_peer(1))
+
+    @pl.when(has_left)
+    def _():
+        halo_done(halo_left, hr_send, hl_recv).wait_recv()
+
+    @pl.when(jnp.logical_not(has_left))
+    def _():
+        halo_left[...] = jnp.zeros_like(halo_left)
+
+    @pl.when(has_right)
+    def _():
+        halo_done(halo_right, hl_send, hr_recv).wait_recv()
+
+    @pl.when(jnp.logical_not(has_right))
+    def _():
+        halo_right[...] = jnp.zeros_like(halo_right)
+
+    _, left = image_of(sum([twice(g, halo_left[g]) for g in range(groups)], []))
+    right, _ = image_of(sum([twice(g, halo_right[g]) for g in range(groups)], []))
     for c in range(count - 1):
         finish(c)
 
-    def halo_done(ref, send, recv):
-        return remote(ref, ref, send, recv, freq=freq_peer(1))
-
-    @pl.when(has_left)
-    def _():
-        halo_done(halo_left, hr_send, hl_recv).wait_recv()
-
-    @pl.when(jnp.logical_not(has_left))
-    def _():
-        halo_left[...] = jnp.zeros_like(halo_left)
-
-    @pl.when(has_right)
-    def _():
-        halo_done(halo_right, hl_send, hr_recv).wait_recv()
-
-    @pl.when(jnp.logical_not(has_right))
-    def _():
-        halo_right[...] = jnp.zeros_like(halo_right)
-
-    _, left = image_of(twice([halo_left[g] for g in range(groups)]))
-    right, _ = image_of(twice([halo_right[g] for g in range(groups)]))
     def smooth(at, end):
         if at >= end:
             return
@@ -609,6 +651,10 @@
     short, long, squeeze = series_tables(groups, bins_dev, time_dev, probes)
     img_tab, inner, each, slot = image_tables(groups, bins_dev, time_dev, keep)
     tabs = np.concatenate([long, inner], axis=1)
+    main = sens_dev // LANES
+    fit = LANES // (sens_dev - main * LANES)
+    assert squeeze * probes % PAIR == 0
+    lines = main * squeeze * probes + -(-squeeze * probes // PAIR // fit) * PAIR
     tabs = np.tile(tabs, (1, 1, STEP // bins_dev)).astype(np.float32)
     unit = (2 * each, LANES)
     dma = pltpu.SemaphoreType.DMA
@@ -629,8 +675,8 @@
             pltpu.VMEM(tabs.shape[1:], F32),
             pltpu.VMEM(img_tab.shape[1:], BF16),
             pltpu.VMEM((2, slot, STEP), F32),
-            pltpu.VMEM((groups, squeeze * probes, sens_dev), BF16),
-            pltpu.VMEM((groups, squeeze * probes, sens_dev), BF16),
+            pltpu.VMEM((groups, lines, LANES), BF16),
+            pltpu.VMEM((groups, lines, LANES), BF16),
             pltpu.VMEM((sens_dev, padded), BF16),
             pltpu.VMEM((2, probes, padded), F32),
             pltpu.VMEM((senses * slot, 2 * padded), BF16),
@@ -645,7 +691,7 @@
             pltpu.VMEM((groups,) + unit, BF16),
             pltpu.VMEM((groups,) + unit, BF16),
             dma((6,)),
-            dma((count, 2)),
+            dma((count,)),
             dma,
             dma,
             dma,

time: 19.2 us -> 18.7 us (0.974)
  Pallas kernels: 18.3 us -> 17.9 us
    pallas_call x1, Pallas kernels: 18.3 us -> 17.9 us  [local(): pl.pallas_call(functools.partial(body, (groups, params, senses, chunks, d...]
where the time goes in v5:
time: 18.7 us; the launch traced here: 18.6 us
  Pallas kernels  17.9 us (96%)
  local copies, waits for them, and re-layouts  0.69 us (4%)
    pallas_call x1, Pallas kernels, local(): pl.pallas_call(functools.partial(body, (groups, params, senses, chunks, d...  17.9 us
    unnamed x1, local copies, waits for them, and re-layouts  0.69 us

profile of v5, /device:TPU:0, one launch (start us, length us, event | category | flops | bytes accessed | tf_op | source)
XLA Modules:
  0.0 18.6 jit_solution(4021430131792538695)
XLA Ops:
  0.0 17.9 %shard_map.73 = f32[26,2,1024]{2,1,0:T(2,128)S(1)} custom-call(bf16[208,150]{1,0:T(8,128)(2,1)} %bitcast.8, bf16[2,2400,1024]{2,1,0:T(8,128)(2,1)} %bitcast.7, f32[16]{0:T(128)} %prior_hbm.1, f32[1,1024]{1,0:T(1,128)} %bitcast.9, bf16[2,2,80,208]{3,2,1,0:T(8,128)(2,1)} %constant.6.clone.short_hbm, f32[2,104,256]{2,1,0:T(8,128)} %constant.7.clone.tabs_hbm, ...), custom_call_target="tpu_custom_call" | custom-call | tf_op jit(solution)/shard_map/pallas_call | solution.py:662
  17.9 0.7 %copy.9 = f32[26,2,1024]{2,1,0:T(2,128)} copy(f32[26,2,1024]{2,1,0:T(2,128)S(1)} %shard_map.73) | data formatting | bytes 425984

commit v6 on v5

--- a/solution.py
+++ b/solution.py
@@ -57,7 +57,7 @@
     parts = [factor(block.reshape(-1, time_dev), 2) for block in blocks]
     rank = max(part[2] for part in parts)
     short = np.stack([right[:rank] for _, right, _ in parts])
-    short = np.stack(split(with_probes(short, probes)), axis=1)
+    short = np.concatenate(split(with_probes(short, probes)), axis=1)
     long = np.stack([left[:, :rank] for left, _, _ in parts])
     long = long.reshape(groups, groups, 2, bins_dev, rank).transpose(0, 1, 2, 4, 3)
     long = np.stack([np.roll(long[g], -g, axis=0) for g in range(groups)])
@@ -85,8 +85,7 @@
     for half, places in enumerate(packing(each)):
         packed[:, :, half * tall : half * tall + rows, places] = full
     high, low = split(packed)
-    own = np.stack([high[g, g] for g in range(groups)])
-    image = np.concatenate([high, low, own[:, None]], axis=1)
+    image = np.concatenate([high, low], axis=2)
     inner = np.stack([right[:rank] for _, right, _ in parts])
     inner = inner.reshape(groups, rank, 2, bins_dev).transpose(0, 2, 1, 3)
     inner = np.repeat(inner, keep, axis=2)
@@ -145,7 +144,7 @@
     ready_z,
     ready_far,
 ):
-    groups, params, senses, chunks, direct, bins_dev, probes, squeeze, each = cfg
+    groups, params, senses, chunks, joint, direct, bins_dev, probes, squeeze, each = cfg
     f = lax.axis_index("freq")
     k = lax.axis_index("param")
     s = lax.axis_index("sens")
@@ -219,13 +218,14 @@
     loads = [
         [
             pltpu.make_async_copy(
-                kernel_hbm.at[part, :, pl.ds(at, width)],
-                kbufs[c].at[pl.ds(part * padded, depth)],
-                k_sem.at[c],
+                kernel_hbm.at[part, :, pl.ds(chunks[c], width)],
+                kbufs[i].at[pl.ds(part * padded, depth), pl.ds(n * width, width)],
+                k_sem.at[i],
             )
+            for n, c in enumerate(some)
             for part in range(2)
         ]
-        for c, at in enumerate(chunks)
+        for i, some in enumerate(joint)
     ]
     for group in loads:
         for copy in group:
@@ -234,9 +234,8 @@
     series = rows[...]
 
     def shortened(g):
-        return jnp.dot(short[g, 0], series, preferred_element_type=F32) + jnp.dot(
-            short[g, 1], series, preferred_element_type=F32
-        )
+        both = jnp.dot(short[g], series, preferred_element_type=F32)
+        return both[: squeeze * probes] + both[squeeze * probes :]
 
     main = sens_dev // LANES * LANES
     rest = sens_dev - main
@@ -331,9 +330,9 @@
     def _():
         tell(ready_far, sens=pair)
 
-    def loaded(c):
-        part = kbufs[c].at[pl.ds(0, 2 * depth)]
-        pltpu.make_async_copy(part, part, k_sem.at[c]).wait()
+    def loaded(i):
+        part = kbufs[i].at[pl.ds(0, 2 * depth)]
+        pltpu.make_async_copy(part, part, k_sem.at[i]).wait()
 
     loaded(0)
 
@@ -469,27 +468,28 @@
         return total
 
     whole = each // 8 * 8
-    for c in range(count):
-        if c > 0:
-            loaded(c)
+    for i, some in enumerate(joint):
         total = head
-        if c > 0:
-            total = jnp.dot(left_mat[...], kbufs[c][...], preferred_element_type=F32)
-        for j in range(senses):
-            halves = [
-                total[j * slot : (j + 1) * slot, h * LANES : (h + 1) * LANES] for h in range(2)
-            ]
-            packed = [half[:whole] for half in halves]
-            if slot > each:
-                packed.append(halves[0][whole:] + pltpu.roll(halves[1][whole:], each - whole, 0))
-            sbuf[j, c] = jnp.concatenate(packed, axis=0).astype(BF16)
-        if c == 0:
+        if i > 0:
+            loaded(i)
+            total = jnp.dot(left_mat[...], kbufs[i][...], preferred_element_type=F32)
+        for n, c in enumerate(some):
+            for j in range(senses):
+                block = total[j * slot : (j + 1) * slot, n * width : (n + 1) * width]
+                halves = [block[:, h * LANES : (h + 1) * LANES] for h in range(2)]
+                packed = [half[:whole] for half in halves]
+                if slot > each:
+                    turned = pltpu.roll(halves[1][whole:], each - whole, 0)
+                    packed.append(halves[0][whole:] + turned)
+                sbuf[j, c] = jnp.concatenate(packed, axis=0).astype(BF16)
+        if i == 0:
 
             @pl.when(outer)
             def _():
                 pl.semaphore_wait(ready_far, 1)
 
-        send_sums(c)
+        for c in some:
+            send_sums(c)
 
     def x_copy(target, c):
         part = gath.at[f, c]
@@ -520,29 +520,26 @@
         )
 
     rows_out = scaled.shape[0]
-    tall = img_tab.shape[1] // 2
-
-    def image_of(pieces):
+    tall = img_tab.shape[1] // 4
+
+    def image_of(pieces, lower=None):
         total = None
-        for index, piece in pieces:
-            term = jnp.dot(img_tab[index], piece, preferred_element_type=F32)
+        for g, piece in pieces:
+            term = jnp.dot(img_tab[g], piece, preferred_element_type=F32)
             total = term if total is None else total + term
+        total = total[: 2 * tall] + total[2 * tall :]
+        if lower is not None:
+            total = total + jnp.dot(img_tab[f, : 2 * tall], lower, preferred_element_type=F32)
         return total[:rows_out], total[tall : tall + rows_out]
 
-    def twice(g, piece):
-        return [(g, piece), (groups + g, piece)]
-
     def begin(c):
-        pieces = twice(f, gath[f, c]) + [(2 * groups, lows[c])]
-        for half, image in enumerate(image_of(pieces)):
+        for half, image in enumerate(image_of([(f, gath[f, c])], lows[c])):
             at = chunks[c] + half * LANES
             scaled[:, at : at + LANES] = image
 
     def finish(c):
         x_done(c).wait_recv()
-        pieces = []
-        for d in range(1, groups):
-            pieces += twice(freq_peer(d), gath[freq_peer(d), c])
+        pieces = [(freq_peer(d), gath[freq_peer(d), c]) for d in range(1, groups)]
         for half, image in enumerate(image_of(pieces)):
             at = chunks[c] + half * LANES
             lanes = slice(at, at + LANES)
@@ -596,8 +593,8 @@
     def _():
         halo_right[...] = jnp.zeros_like(halo_right)
 
-    _, left = image_of(sum([twice(g, halo_left[g]) for g in range(groups)], []))
-    right, _ = image_of(sum([twice(g, halo_right[g]) for g in range(groups)], []))
+    _, left = image_of([(g, halo_left[g]) for g in range(groups)])
+    right, _ = image_of([(g, halo_right[g]) for g in range(groups)])
     for c in range(count - 1):
         finish(c)
 
@@ -644,7 +641,8 @@
     assert cols % width == 0
     chunks = list(range(0, cols, width))
     chunks = chunks[:1] + chunks[:0:-1][:1] + chunks[1:-1]
-    direct = (len(chunks) - 1,)
+    direct = tuple(range(len(chunks) // 2, len(chunks)))
+    joint = [[0], list(range(1, len(chunks) - 1)), [len(chunks) - 1]]
     count = len(chunks)
     depth = sens_dev * bins_dev
     padded = -(-depth // LANES) * LANES
@@ -661,13 +659,13 @@
     plain = pltpu.SemaphoreType.REGULAR
     return pl.pallas_call(
         functools.partial(
-            body, (groups, params, senses, chunks, direct, bins_dev, probes, squeeze, each)
+            body, (groups, params, senses, chunks, joint, direct, bins_dev, probes, squeeze, each)
         ),
         out_shape=pltpu.VMEM((time_dev, keep, cols), F32),
         in_specs=[pl.BlockSpec(memory_space=pltpu.HBM)] * 7,
         out_specs=pl.BlockSpec(memory_space=pltpu.VMEM),
         scratch_shapes=[
-            [pltpu.VMEM((2 * padded, width), BF16) for _ in chunks],
+            [pltpu.VMEM((2 * padded, width * len(some)), BF16) for some in joint],
             pltpu.VMEM((time_dev * probes, sens_dev), BF16),
             pltpu.SMEM((bins_dev,), F32),
             pltpu.VMEM((1, cols), F32),
@@ -691,12 +689,12 @@
             pltpu.VMEM((groups,) + unit, BF16),
             pltpu.VMEM((groups,) + unit, BF16),
             dma((6,)),
-            dma((count,)),
+            dma((len(joint),)),
             dma,
             dma,
             dma,
             dma((count,)),
-            dma((count,)),
+            dma((count - len(direct),)),
             dma,
             dma((count,)),
             dma,

time: 18.7 us -> 18.4 us (0.984)
  Pallas kernels: 17.9 us -> 17.6 us
    pallas_call x1, Pallas kernels: 17.9 us -> 17.6 us  [local(): pl.pallas_call(functools.partial(body, (groups, params, senses, chunks, j...]
where the time goes in v6:
time: 18.4 us; the launch traced here: 18.3 us
  Pallas kernels  17.6 us (96%)
  local copies, waits for them, and re-layouts  0.69 us (4%)
    pallas_call x1, Pallas kernels, local(): pl.pallas_call(functools.partial(body, (groups, params, senses, chunks, j...  17.6 us
    unnamed x1, local copies, waits for them, and re-layouts  0.69 us

profile of v6, /device:TPU:0, one launch (start us, length us, event | category | flops | bytes accessed | tf_op | source)
XLA Modules:
  0.0 18.3 jit_solution(15900316128709253045)
XLA Ops:
  0.0 17.6 %shard_map.73 = f32[26,2,1024]{2,1,0:T(2,128)S(1)} custom-call(bf16[208,150]{1,0:T(8,128)(2,1)} %bitcast.8, bf16[2,2400,1024]{2,1,0:T(8,128)(2,1)} %bitcast.7, f32[16]{0:T(128)} %prior_hbm.1, f32[1,1024]{1,0:T(1,128)} %bitcast.9, bf16[2,160,208]{2,1,0:T(8,128)(2,1)} %constant.6.clone.short_hbm, f32[2,104,256]{2,1,0:T(8,128)} %constant.7.clone.tabs_hbm, ...), custom_call_target="tpu_custom_call" | custom-call | tf_op jit(solution)/shard_map/pallas_call | solution.py:660
  17.6 0.7 %copy.9 = f32[26,2,1024]{2,1,0:T(2,128)} copy(f32[26,2,1024]{2,1,0:T(2,128)S(1)} %shard_map.73) | data formatting | bytes 425984

commit v7 on v6

--- a/solution.py
+++ b/solution.py
@@ -421,22 +421,27 @@
             joined.at[c], rbuf.at[s, c], z_send, z_recv.at[c], sens=across
         )
 
-    def send_sums(c):
+    def send_far(c):
         if c in direct:
-            for target in (across, other, pair):
-                z_copy(target, c).start()
+            z_copy(across, c).start()
+            if c == count - 1:
+                z_copy(other, c).start()
+                return
+
+            @pl.when(within)
+            def _():
+                z_copy(other, c).start()
+
             return
 
         @pl.when(outer)
         def _():
+            relay_copy(c).start()
             z_copy(across, c).start()
-            relay_copy(c).start()
-            z_copy(pair, c).start()
 
         @pl.when(within)
         def _():
             z_copy(other, c).start()
-            z_copy(pair, c).start()
 
     def pass_on(c):
         if c in direct:
@@ -489,7 +494,14 @@
                 pl.semaphore_wait(ready_far, 1)
 
         for c in some:
-            send_sums(c)
+            send_far(c)
+        if i == 0 or i == len(joint) - 1:
+            late = [c for part in joint[min(i, 1) : i + 1] for c in part]
+            for c in late:
+                if c in direct and c < count - 1:
+                    pl.when(outer)(z_copy(other, c).start)
+            for c in late:
+                z_copy(pair, c).start()
 
     def x_copy(target, c):
         part = gath.at[f, c]

time: 18.4 us -> 18.4 us (level)
  no operation moved by 1% of the time
where the time goes in v7:
time: 18.4 us; the launch traced here: 18.3 us
  Pallas kernels  17.6 us (96%)
  local copies, waits for them, and re-layouts  0.69 us (4%)
    pallas_call x1, Pallas kernels, local(): pl.pallas_call(functools.partial(body, (groups, params, senses, chunks, j...  17.6 us
    unnamed x1, local copies, waits for them, and re-layouts  0.69 us

profile of v7, /device:TPU:0, one launch (start us, length us, event | category | flops | bytes accessed | tf_op | source)
XLA Modules:
  0.0 18.3 jit_solution(4981516668141508848)
XLA Ops:
  0.0 17.6 %shard_map.73 = f32[26,2,1024]{2,1,0:T(2,128)S(1)} custom-call(bf16[208,150]{1,0:T(8,128)(2,1)} %bitcast.8, bf16[2,2400,1024]{2,1,0:T(8,128)(2,1)} %bitcast.7, f32[16]{0:T(128)} %prior_hbm.1, f32[1,1024]{1,0:T(1,128)} %bitcast.9, bf16[2,160,208]{2,1,0:T(8,128)(2,1)} %constant.6.clone.short_hbm, f32[2,104,256]{2,1,0:T(8,128)} %constant.7.clone.tabs_hbm, ...), custom_call_target="tpu_custom_call" | custom-call | tf_op jit(solution)/shard_map/pallas_call | solution.py:672
  17.6 0.7 %copy.9 = f32[26,2,1024]{2,1,0:T(2,128)} copy(f32[26,2,1024]{2,1,0:T(2,128)S(1)} %shard_map.73) | data formatting | bytes 425984
